TPU v7x, 32 devices: a whole 2x2x4 slice. The times are simulated.
32 devices in a mesh: egrp: 8 (over y, x, core), eloc: 4 (over z).
Axes of the slice: x: 2, y: 2, z: 4, core: 2. Of those that a mesh axis runs over, the one named last changes fastest.
Arguments:
- green_blocks: bfloat16 [32, 16, 3, 64, 128], P(('egrp', 'eloc')), may hold values from -0.3125 to 0.3125
- sigma_prev: bfloat16 [32, 16, 64, 128], P(('egrp', 'eloc')), may hold values from -6 to 6
- neighbours: int32 [16, 2], replicated, may hold values from 0 to 15
- couplings: bfloat16 [6, 16, 64, 128], P(None, 'eloc'), may hold values from -0.375 to 0.375
- occupancy: float32 [6], replicated, may hold values from 0.1 to 2
- shifts: int32 [6], replicated, may hold values from 1 to 4, as said below
Outputs:
- sigma_next: bfloat16 [32, 16, 64, 128], P(('egrp', 'eloc'))
Inputs may be any that keep to these rules, and one draw needn't show every extreme that they name: `shifts`: at least one mode's shift equals 4.
All inputs are finite; a program needn't handle non-finite values.
Results may differ from a plain program's by a relative error of at most 0.0065.
Values may be sent and summed in bfloat16 or wider, within the bound.
No kernel may reach another device: no remote copies, remote signals or barrier semaphores. Data moves between devices by JAX's collectives and lax.ppermute only.
A program may use at most 64 MiB of HBM per device.

v0:
```python
import jax
import jax.numpy as jnp
from jax import lax
from jax.sharding import PartitionSpec as P


def extended_2(cells, sides, width):
    for axis, dim in sides:
        count = lax.axis_size(axis)
        ends = count - 1
        head = lax.slice_in_dim(cells, 0, width, axis=dim)
        tail = lax.slice_in_dim(cells, cells.shape[dim] - width, cells.shape[dim], axis=dim)
        cells = jnp.concatenate(
            [
                lax.ppermute(tail, axis, [(i, (i + 1) % count) for i in range(ends)]),
                cells,
                lax.ppermute(head, axis, [((i + 1) % count, i) for i in range(ends)]),
            ],
            axis=dim,
        )
    return cells


def widened_form(block):
    orbitals = block.shape[-2]
    real_part = block[..., :orbitals]
    imag_part = block[..., orbitals:]
    upper_rows = jnp.concatenate([real_part, imag_part], -1)
    lower_rows = jnp.concatenate([-imag_part, real_part], -1)
    return jnp.concatenate([upper_rows, lower_rows], -2)


def adjoint_form(block):
    orbitals = block.shape[-2]
    real_part = jnp.swapaxes(block[..., :orbitals], -1, -2)
    imag_part = jnp.swapaxes(block[..., orbitals:], -1, -2)
    upper_rows = jnp.concatenate([real_part, -imag_part], -1)
    lower_rows = jnp.concatenate([imag_part, real_part], -1)
    return jnp.concatenate([upper_rows, lower_rows], -2)


def shards(green_blocks, sigma_prev, neighbours, couplings, occupancy, shifts):
    blocks = green_blocks[0]
    sigma_local = sigma_prev[0]
    atom_count = blocks.shape[0]
    atom_index = jnp.concatenate([jnp.arange(atom_count, dtype=jnp.int32)[:, None], neighbours], 1)
    chosen = jnp.take(sigma_local, atom_index, axis=0)
    half_product = jnp.einsum(
        "akij,akjl->akil", blocks, widened_form(chosen), preferred_element_type=jnp.float32
    ).astype(jnp.bfloat16)
    lesser = jnp.einsum(
        "akij,akjl->ail", half_product, adjoint_form(blocks), preferred_element_type=jnp.float32
    )
    regrouped = lax.all_to_all(lesser[None], "eloc", split_axis=1, concat_axis=0, tiled=True)
    group_size = regrouped.shape[0]
    mode_count = couplings.shape[0]
    coupling_float = couplings.astype(jnp.float32)
    right_forms = adjoint_form(coupling_float)
    extended = extended_2(regrouped, (("egrp", 0),), group_size)
    self_energy = jnp.zeros_like(regrouped)
    for mode_index in range(mode_count):
        shift_now = shifts[mode_index]
        upper_part = lax.dynamic_slice_in_dim(extended, group_size + shift_now, group_size, 0)
        lower_part = lax.dynamic_slice_in_dim(extended, group_size - shift_now, group_size, 0)
        mixture = (occupancy[mode_index] + 1.0) * upper_part + occupancy[mode_index] * lower_part
        left = jnp.einsum(
            "aij,eajl->eail",
            coupling_float[mode_index],
            widened_form(mixture),
            precision=lax.Precision.HIGHEST,
        )
        self_energy = self_energy + jnp.einsum(
            "eaij,ajl->eail", left, right_forms[mode_index], precision=lax.Precision.HIGHEST
        )
    result = self_energy.astype(jnp.bfloat16)
    return lax.all_to_all(result, "eloc", split_axis=0, concat_axis=1, tiled=True)


def solution(mesh):
    return jax.shard_map(
        shards,
        mesh=mesh,
        in_specs=(
            P(("egrp", "eloc"), None, None, None, None),
            P(("egrp", "eloc"), None, None, None),
            P(),
            P(None, "eloc", None, None),
            P(),
            P(),
        ),
        out_specs=P(("egrp", "eloc"), None, None, None),
        check_vma=False,
    )
```

profile of v0, /device:TPU:4, one launch (start us, length us, event | category | flops | bytes accessed | tf_op | source)
XLA Modules:
  0.0 80.6 jit_solution(2139949568907967210)
XLA Ops:
  0.0 1.8 %copy.26 = bf16[1,16,3,64,128]{3,4,2,1,0:T(8,128)(2,1)S(1)} copy(bf16[1,16,3,64,128]{4,3,2,1,0:T(8,128)(2,1)} %param.6) | data formatting | bytes 1572864 | tf_op args[0]
  1.8 1.3 %slice_bitcast_fusion = (bf16[16,3,64,64]{3,2,1,0:T(8,128)(2,1)}, bf16[16,3,64,64]{3,2,1,0:T(8,128)(2,1)}) fusion(bf16[16,3,64,128]{2,3,1,0:T(8,128)(2,1)S(1)} %bitcast.157), kind=kLoop, calls=%fused_computation.62 | loop fusion | bytes 1572864 | tf_op jit(solution)/shard_map/transpose | solution.py:36
  3.5 0.7 gather_fusion
  4.3 1.7 %slice_negate_fusion = (bf16[16,3,64,64]{3,2,1,0:T(8,128)(2,1)}, bf16[16,3,64,64]{3,2,1,0:T(8,128)(2,1)}, bf16[16,3,64,64]{3,2,1,0:T(8,128)(2,1)}) fusion(bf16[16,3,64,128]{3,2,1,0:T(8,128)(2,1)S(1)} %broadcast_select_fusion, bf16[16,3,64,128]{2,3,1,0:T(8,128)(2,1)S(1)} %bitcast.158), kind=kLoop, calls=%fused_computation.64 | loop fusion | flops 393216 | bytes 2359296 | tf_op jit(solution)/shard_map/neg | solution.py:29
  6.1 5.0 %fusion.20 = f32[1,16,64,128]{3,2,0,1:T(8,128)} fusion(bf16[16,3,64,64]{3,2,1,0:T(8,128)(2,1)} %get-tuple-element.14, bf16[16,3,64,64]{3,2,1,0:T(8,128)(2,1)} %get-tuple-element.13, bf16[16,3,64,64]{3,2,1,0:T(8,128)(2,1)} %get-tuple-element.41, bf16[16,3,64,64]{3,2,1,0:T(8,128)(2,1)} %get-tuple-element.16, bf16[16,3,64,64]{3,2,1,0:T(8,128)(2,1)} %get-tuple-element.15, ...), kind=kOutput, calls=%fused_computation.18 | convolution fusion | flops 212729856 | bytes 4063232 | tf_op jit(solution)/shard_map/akij,akjl->ail/dot_general | solution.py:51
  11.1 4.9 %all-to-all-start = ((f32[1,16,64,128]{3,2,0,1:T(8,128)}), f32[1,16,64,128]{3,2,0,1:T(8,128)S(1)}, u32[]{:S(2)}, u32[]{:S(2)}) async-start(f32[1,16,64,128]{3,2,0,1:T(8,128)} %fusion.20), calls=%async_computation | async-start | bytes 1048576 | tf_op jit(solution)/shard_map/all_to_all | solution.py:54
  16.0 0.7 fusion.83
  32.7 0.8 %copy.29 = f32[4,4,64,128]{3,2,0,1:T(8,128)} copy(f32[4,4,64,128]{3,2,1,0:T(8,128)S(1)} %bitcast.159) | data formatting | bytes 1048576 | tf_op jit(solution)/shard_map/all_to_all | solution.py:54
  33.5 1.9 %collective-permute-start = (f32[4,4,64,128]{3,2,0,1:T(8,128)}, f32[4,4,64,128]{3,2,0,1:T(8,128)}, u32[]{:S(2)}, u32[]{:S(2)}) collective-permute-start(f32[4,4,64,128]{3,2,0,1:T(8,128)} %copy.29), channel_id=1, source_target_pairs={{0,4},{4,8},{8,12},{12,16},{16,20},{20,24},{24,28},{1,5},{5,9},{9,... | collective-permute-start | bytes 1572872 | tf_op jit(solution)/shard_map/ppermute | solution.py:15
  35.5 0.7 fusion.82
  40.2 4.7 %collective-permute-start.1 = (f32[4,4,64,128]{3,2,0,1:T(8,128)}, f32[4,4,64,128]{3,2,0,1:T(8,128)S(1)}, u32[]{:S(2)}, u32[]{:S(2)}) collective-permute-start(f32[4,4,64,128]{3,2,0,1:T(8,128)} %copy.29), channel_id=1, source_target_pairs={{4,0},{8,4},{12,8},{16,12},{20,16},{24,20},{28,24},{5,1},{9,5},{13... | collective-permute-start | bytes 1572872 | tf_op jit(solution)/shard_map/ppermute | solution.py:17
  45.5 1.1 %constant_dynamic-update-slice_fusion.2 = f32[12,4,64,128]{3,2,0,1:T(8,128)S(1)} fusion(f32[4,4,64,128]{3,2,0,1:T(8,128)} %collective-permute-done), kind=kLoop, calls=%fused_computation.102 | loop fusion | bytes 1048576
  46.6 5.2 %collective-permute-done.1 = f32[4,4,64,128]{3,2,0,1:T(8,128)S(1)} collective-permute-done((f32[4,4,64,128]{3,2,0,1:T(8,128)}, f32[4,4,64,128]{3,2,0,1:T(8,128)S(1)}, u32[]{:S(2)}, u32[]{:S(2)}) %collective-permute-start.1) | collective-permute-done | bytes 524320 | tf_op jit(solution)/shard_map/ppermute | solution.py:17
  51.8 1.6 %multiply_add_fusion.1 = (f32[4,4,64,128]{3,2,0,1:T(8,128)S(1)}, f32[4,4,64,128]{3,2,0,1:T(8,128)S(1)}) fusion(f32[12,4,64,128]{3,2,0,1:T(8,128)S(1)} %constant_dynamic-update-slice_fusion, s32[]{:T(128)S(6)} %select_n.68, s32[]{:T(128)S(6)} %select_n.67, f32[]{:T(128)} %bitcast.66, f32[]{:T(128)S(6)} %add.237, s32[]{:T(128)S(6)} %select_n.60, f32[]{:T(128)} %bitcast.5, ...), kind=kLoop, calls=%fused_computation.76 | loop fusion | flops 786432 | bytes 3145760 | tf_op jit(solution)/shard_map/add | solution.py:65
  53.7 3.1 %multiply_add_fusion = (f32[4,4,64,128]{3,2,0,1:T(8,128)S(1)}, f32[4,4,64,128]{3,2,0,1:T(8,128)S(1)}, f32[4,4,64,128]{3,2,0,1:T(8,128)S(1)}, f32[4,4,64,128]{3,2,0,1:T(8,128)S(1)}) fusion(f32[12,4,64,128]{3,2,0,1:T(8,128)S(1)} %constant_dynamic-update-slice_fusion, s32[]{:T(128)S(6)} %select_n.70, s32[]{:T(128)S(6)} %select_n.69, f32[]{:T(128)} %bitcast.78, ...), kind=kLoop, calls=%fused_computation.75 | loop fusion | flops 1572864 | bytes 6291520 | tf_op jit(solution)/shard_map/add | solution.py:65
  57.9 0.6 convolution_bitcast_fusion.5
  59.1 0.6 convolution_bitcast_fusion.4
  60.3 0.6 convolution_bitcast_fusion.3
  61.5 0.6 convolution_bitcast_fusion.2
  62.7 0.6 convolution_bitcast_fusion.1
  63.9 0.6 convolution_bitcast_fusion
  64.5 0.6 fusion.24
  65.2 14.7 %all_to_all.24 = bf16[4,4,64,128]{3,2,1,0:T(8,128)(2,1)S(1)} all-to-all(bf16[4,4,64,128]{3,2,1,0:T(8,128)(2,1)S(1)} %copy.32), channel_id=1, replica_groups=mesh['egrp'=8,'eloc'=4] {'eloc'}, dimensions={0} | all-to-all | bytes 524288 | tf_op jit(solution)/shard_map/all_to_all | solution.py:76
  79.9 0.7 copy.53
  (40 shorter events, 6.0 us)
Async XLA Ops:
  0.0 3.5 %copy-start = (bf16[1,16,64,128]{3,2,1,0:T(8,128)(2,1)S(1)}, bf16[1,16,64,128]{3,2,1,0:T(8,128)(2,1)}, u32[]{:S(2)}) copy-start(bf16[1,16,64,128]{3,2,1,0:T(8,128)(2,1)} %param.7) | copy-start | bytes 786436
  1.8 1.3 %copy-start.4 = (s32[16,2]{0,1:T(2,128)S(1)}, s32[16,2]{0,1:T(2,128)}, u32[]{:S(2)}) copy-start(s32[16,2]{0,1:T(2,128)} %param.8) | copy-start | bytes 388
  6.1 9.9 %copy-start.2 = (s32[6]{0:T(128)S(1)}, s32[6]{0:T(128)}, u32[]{:S(2)}) copy-start(s32[6]{0:T(128)} %param.11) | copy-start | bytes 76
  6.1 25.9 %copy-start.1 = (bf16[6,4,64,128]{3,2,1,0:T(8,128)(2,1)S(1)}, bf16[6,4,64,128]{3,2,1,0:T(8,128)(2,1)}, u32[]{:S(2)}) copy-start(bf16[6,4,64,128]{3,2,1,0:T(8,128)(2,1)} %param.9) | copy-start | bytes 1179652
  11.1 21.6 %all-to-all-start = ((f32[1,16,64,128]{3,2,0,1:T(8,128)}), f32[1,16,64,128]{3,2,0,1:T(8,128)S(1)}, u32[]{:S(2)}, u32[]{:S(2)}) async-start(f32[1,16,64,128]{3,2,0,1:T(8,128)} %fusion.20), calls=%async_computation | async-start | bytes 1048576 | tf_op jit(solution)/shard_map/all_to_all | solution.py:54
  32.6 2.9 %copy-start.3 = (f32[6]{0:T(128)S(1)}, f32[6]{0:T(128)}, u32[]{:S(2)}) copy-start(f32[6]{0:T(128)} %param.10) | copy-start | bytes 76
  33.5 11.9 %collective-permute-start = (f32[4,4,64,128]{3,2,0,1:T(8,128)}, f32[4,4,64,128]{3,2,0,1:T(8,128)}, u32[]{:S(2)}, u32[]{:S(2)}) collective-permute-start(f32[4,4,64,128]{3,2,0,1:T(8,128)} %copy.29), channel_id=1, source_target_pairs={{0,4},{4,8},{8,12},{12,16},{16,20},{20,24},{24,28},{1,5},{5,9},{9,... | collective-permute-start | bytes 1572872 | tf_op jit(solution)/shard_map/ppermute | solution.py:15
  40.2 11.5 %collective-permute-start.1 = (f32[4,4,64,128]{3,2,0,1:T(8,128)}, f32[4,4,64,128]{3,2,0,1:T(8,128)S(1)}, u32[]{:S(2)}, u32[]{:S(2)}) collective-permute-start(f32[4,4,64,128]{3,2,0,1:T(8,128)} %copy.29), channel_id=1, source_target_pairs={{4,0},{8,4},{12,8},{16,12},{20,16},{24,20},{28,24},{5,1},{9,5},{13... | collective-permute-start | bytes 1572872 | tf_op jit(solution)/shard_map/ppermute | solution.py:17
where the time goes:
time: 81.2 us; the launch traced here: 80.6 us
  between operations  19.6 us (24%)
  blocking collectives  14.7 us (18%)
  matrix products  12.2 us (15%)
  starting transfers between devices  11.5 us (14%)
  local copies, waits for them, and re-layouts  8.7 us (11%)
  other arithmetic  8.64 us (11%)
  waiting for transfers between devices  5.2 us (6%)
    all_to_all x1, blocking collectives, shards(): lax.all_to_all(result, 'eloc', split_axis=0, concat_axis=1, tiled=True)  14.7 us
    ppermute x1, waiting for transfers between devices, extended_2(): lax.ppermute(head, axis, [((i + 1) % count, i) for i in range(ends)])  5.2 us
    dot_general x1, matrix products, shards(): jnp.einsum('akij,akjl->ail', half_product, adjoint_form(blocks), preferre...  5.04 us
    all_to_all x1, starting transfers between devices, shards(): lax.all_to_all(lesser[None], 'eloc', split_axis=1, concat_axis=0, tiled=T...  4.86 us
    add x2, other arithmetic, shards(): (occupancy[mode_index] + 1.0) * upper_part  4.77 us
    ppermute x1, starting transfers between devices, extended_2(): lax.ppermute(head, axis, [((i + 1) % count, i) for i in range(ends)])  4.72 us
    unnamed x15, local copies, waits for them, and re-layouts  4.05 us
    dot_general x6, matrix products, shards(): jnp.einsum('aij,eajl->eail', coupling_float[mode_index], widened_form(mix...  3.6 us
  transfers between devices with their start and end apart: 3, of which 1 were waited for; matrix products, arithmetic and copies ran while one was open for 5% of the time, Pallas kernels for 0%

commit v1 on v0

v1 whole, which is shorter than its diff:
```python
import jax
import jax.numpy as jnp
from jax import lax
from jax.experimental import pallas as pl
from jax.experimental.pallas import tpu as pltpu
from jax.sharding import PartitionSpec as P

VMEM = pl.BlockSpec(memory_space=pltpu.VMEM)
SMEM = pl.BlockSpec(memory_space=pltpu.SMEM)
BF16 = jnp.bfloat16
NT = (((1,), (1,)), ((), ()))


def partner(i, k, n):
    return i ^ k if n & (n - 1) == 0 else (i + k) % n


def source(i, k, n):
    return i ^ k if n & (n - 1) == 0 else (i + n - k) % n


def slot_of(i, j, n):
    return i ^ j if n & (n - 1) == 0 else lax.rem(i - j + n, n)


def target_at(me, k, n):
    return me ^ k if n & (n - 1) == 0 else lax.rem(me + k, n)


def source_at(me, k, n):
    return me ^ k if n & (n - 1) == 0 else lax.rem(me + n - k, n)


def turned(block):
    half = block.shape[-1] // 2
    return jnp.concatenate([-block[:, half:], block[:, :half]], -1)


def lesser_kernel(n, ks, neighbours, green, sigma, *outs):
    me = lax.axis_index("eloc")
    per = outs[0].shape[0]
    for k, out in zip(ks, outs):
        base = target_at(me, k, n) * per
        for i in range(per):
            atom = base + i
            halves, uppers, lowers = [], [], []
            for j in range(green.shape[2]):
                block = green[0, atom, j]
                other = atom if j == 0 else neighbours[atom, j - 1]
                chosen = sigma[0, other]
                wide = jnp.concatenate([chosen, turned(chosen)], 0)
                half = jnp.dot(block, wide, preferred_element_type=jnp.float32)
                halves.append(half.astype(BF16))
                uppers.append(block)
                lowers.append(turned(block))
            left = jnp.concatenate(halves, 1)
            right = jnp.concatenate([jnp.concatenate(uppers, 1), jnp.concatenate(lowers, 1)], 0)
            total = lax.dot_general(left, right, NT, preferred_element_type=jnp.float32)
            out[i] = total.astype(BF16)


def lesser_blocks(n, per, ks, neighbours, green, sigma):
    orb = sigma.shape[-2]

    def kernel(*refs):
        lesser_kernel(n, ks, *refs)

    return pl.pallas_call(
        kernel,
        name="lesser",
        out_shape=[jax.ShapeDtypeStruct((per, orb, 2 * orb), BF16) for _ in ks],
        in_specs=[SMEM, VMEM, VMEM],
        out_specs=[VMEM for _ in ks],
        cost_estimate=pl.CostEstimate(flops=400_000_000, bytes_accessed=2_000_000, transcendentals=0),
    )(neighbours, green, sigma)


def prepare_kernel(occupancy, couplings, right, left):
    modes, per, orb, _ = couplings.shape
    for a in range(per):
        for m in range(modes):
            block = couplings[m, a]
            wide = jnp.concatenate([block, turned(block)], 0).astype(jnp.float32)
            occ = occupancy[m]
            right[a, m, :, : 2 * orb] = (wide * (occ + 1.0)).astype(BF16)
            right[a, m, :, 2 * orb :] = (wide * occ).astype(BF16)
        left[a, :orb] = jnp.concatenate([couplings[m, a][:, :orb] for m in range(modes)], 1)
        left[a, orb:] = jnp.concatenate([couplings[m, a][:, orb:] for m in range(modes)], 1)


def prepared(occupancy, couplings):
    modes, per, orb, _ = couplings.shape
    return pl.pallas_call(
        prepare_kernel,
        name="prepare",
        out_shape=[
            jax.ShapeDtypeStruct((per, modes, 2 * orb, 4 * orb), BF16),
            jax.ShapeDtypeStruct((per, 2 * orb, modes * orb), BF16),
        ],
        in_specs=[SMEM, VMEM],
        out_specs=[VMEM, VMEM],
        cost_estimate=pl.CostEstimate(flops=200_000_000, bytes_accessed=2_000_000, transcendentals=0),
    )(occupancy, couplings)


def modes_kernel(n, ks, shifts, before, here, after, right, left, *rest):
    outs, stack = rest[: len(ks)], rest[-1]
    me = lax.axis_index("eloc")
    per, orb = outs[0].shape[0], outs[0].shape[1]
    modes = right.shape[1]
    width = 2 if len(ks) % 2 == 0 else 1

    def row(t, a):
        slot = slot_of(me, lax.rem(t + n, n), n)
        return slot, t

    for a in range(per):
        for m in range(modes):
            shift = shifts[m]
            rows = []
            for k in ks:
                e = target_at(me, k, n)
                pieces = []
                for t in (e + shift + n, e - shift + n):
                    place = (t // n) * n + slot_of(me, lax.rem(t, n), n)
                    pieces.append(here[place, a])
                rows.append(jnp.concatenate(pieces, 1))
            stacked = jnp.concatenate(rows, 0)
            product = lax.dot_general(stacked, right[a, m], NT, preferred_element_type=jnp.float32)
            product = product.astype(BF16)
            for q in range(len(ks)):
                stack[a, q // width, m * orb : (m + 1) * orb, (q % width) * 2 * orb : (q % width + 1) * 2 * orb] = (
                    product[q * orb : (q + 1) * orb]
                )
        for p in range(len(ks) // width):
            both = jnp.dot(left[a], stack[a, p], preferred_element_type=jnp.float32)
            for w in range(width):
                piece = both[:, w * 2 * orb : (w + 1) * 2 * orb]
                outs[p * width + w][a] = (piece[:orb] + turned(piece[orb:])).astype(BF16)


def mode_blocks(n, ks, shifts, extended, right, left):
    per, modes, wide, _ = right.shape
    orb = wide // 2
    width = 2 if len(ks) % 2 == 0 else 1

    def kernel(shifts, here, right, left, *rest):
        modes_kernel(n, ks, shifts, None, here, None, right, left, *rest)

    return pl.pallas_call(
        kernel,
        name="modes",
        out_shape=[jax.ShapeDtypeStruct((per, orb, 2 * orb), BF16) for _ in ks],
        in_specs=[SMEM, VMEM, VMEM, VMEM],
        out_specs=[VMEM for _ in ks],
        scratch_shapes=[pltpu.VMEM((per, len(ks) // width, modes * orb, width * 2 * orb), BF16)],
        cost_estimate=pl.CostEstimate(flops=400_000_000, bytes_accessed=2_000_000, transcendentals=0),
    )(shifts, extended, right, left)


def join_kernel(n, *refs):
    out = refs[-1]
    me = lax.axis_index("eloc")
    per = refs[0].shape[0]
    for k in range(n):
        out[0, pl.ds(source_at(me, k, n) * per, per)] = refs[k][...]


def joined(n, blocks):
    per, orb, wide = blocks[0].shape

    def kernel(*refs):
        join_kernel(n, *refs)

    return pl.pallas_call(
        kernel,
        name="join",
        out_shape=jax.ShapeDtypeStruct((1, n * per, orb, wide), BF16),
        in_specs=[VMEM for _ in blocks],
        out_specs=VMEM,
    )(*blocks)


def exchanged(n, blocks):
    return [blocks[0]] + [
        lax.ppermute(blocks[k], "eloc", [(i, partner(i, k, n)) for i in range(n)]) for k in range(1, n)
    ]


def shards(green_blocks, sigma_prev, neighbours, couplings, occupancy, shifts):
    n, groups = lax.axis_size("eloc"), lax.axis_size("egrp")
    per = couplings.shape[1]
    ks = tuple(range(n))
    sent = lesser_blocks(n, per, ks, neighbours, green_blocks, sigma_prev)
    right, left = prepared(occupancy, couplings)
    here = jnp.stack(exchanged(n, sent))
    before = lax.ppermute(here, "egrp", [(i, i + 1) for i in range(groups - 1)])
    after = lax.ppermute(here, "egrp", [(i + 1, i) for i in range(groups - 1)])
    extended = jnp.concatenate([before, here, after], 0)
    results = mode_blocks(n, ks, shifts, extended, right, left)
    return joined(n, exchanged(n, results))


def solution(mesh):
    return jax.shard_map(
        shards,
        mesh=mesh,
        in_specs=(
            P(("egrp", "eloc"), None, None, None, None),
            P(("egrp", "eloc"), None, None, None),
            P(),
            P(None, "eloc", None, None),
            P(),
            P(),
        ),
        out_specs=P(("egrp", "eloc"), None, None, None),
        check_vma=False,
    )
```

time: 81.2 us -> 47.7 us (0.59)
  between operations: 19.6 us -> 0.09 us
  blocking collectives: 14.7 us -> 0 us
  Pallas kernels: 0 us -> 13.4 us
  matrix products: 12.2 us -> 0 us
  waiting for transfers between devices: 5.2 us -> 14.4 us
  other arithmetic: 8.64 us -> 0.87 us
  local copies, waits for them, and re-layouts: 8.7 us -> 2.96 us
  starting transfers between devices: 11.5 us -> 15.2 us
    all_to_all x1 -> x0, blocking collectives: 14.7 us -> none  [shards(): lax.all_to_all(result, 'eloc', split_axis=0, concat_axis=1, tiled=True)]
    pallas_call x0 -> x4, Pallas kernels: none -> 13.4 us  [the longest x1 4.54 us: mode_blocks(): pl.pallas_call(kernel, name='modes', out_shape=[jax.ShapeDtypeStruct((per...]
    dot_general x13 -> x0, matrix products: 12.2 us -> none  [the longest x1 5.04 us: shards(): jnp.einsum('akij,akjl->ail', half_product, adjoint_form(blocks), preferre...]
    ppermute x2 -> x8, waiting for transfers between devices: 5.2 us -> 14.4 us  [the longest x6 10.7 us: exchanged(): lax.ppermute(blocks[k], 'eloc', [(i, partner(i, k, n)) for i in range(n)])]
    ppermute x2 -> x8, starting transfers between devices: 6.63 us -> 15.2 us  [the longest x6 8.77 us: exchanged(): lax.ppermute(blocks[k], 'eloc', [(i, partner(i, k, n)) for i in range(n)])]
    all_to_all x1 -> x0, starting transfers between devices: 4.86 us -> none  [shards(): lax.all_to_all(lesser[None], 'eloc', split_axis=1, concat_axis=0, tiled=T...]
    add x2 -> x0, other arithmetic: 4.77 us -> none  [shards(): (occupancy[mode_index] + 1.0) * upper_part]
    neg x8 -> x0, other arithmetic: 3.05 us -> none  [the longest x7 2.98 us: widened_form(): lower_rows = jnp.concatenate([-imag_part, real_part], -1)]
  transfers between devices with their start and end apart: 3 -> 8, of which waited for: 1 -> 6; matrix products, arithmetic and copies ran while one was open for 5% -> 0% of each run, Pallas kernels for 0% -> 6%
where the time goes in v1:
time: 47.7 us; the launch traced here: 46.9 us
  starting transfers between devices  15.2 us (32%)
  waiting for transfers between devices  14.4 us (30%)
  Pallas kernels  13.4 us (28%)
  local copies, waits for them, and re-layouts  2.96 us (6%)
  other arithmetic  0.87 us (2%)
    ppermute x6, waiting for transfers between devices, exchanged(): lax.ppermute(blocks[k], 'eloc', [(i, partner(i, k, n)) for i in range(n)])  10.7 us
    ppermute x6, starting transfers between devices, exchanged(): lax.ppermute(blocks[k], 'eloc', [(i, partner(i, k, n)) for i in range(n)])  8.77 us
    pallas_call x1, Pallas kernels, mode_blocks(): pl.pallas_call(kernel, name='modes', out_shape=[jax.ShapeDtypeStruct((per...  4.54 us
    ppermute x1, starting transfers between devices, shards(): after = lax.ppermute(here, 'egrp', [(i + 1, i) for i in range(groups - 1)])  4.53 us
    pallas_call x1, Pallas kernels, lesser_blocks(): pl.pallas_call(kernel, name='lesser', out_shape=[jax.ShapeDtypeStruct((pe...  4.44 us
    ppermute x1, waiting for transfers between devices, shards(): after = lax.ppermute(here, 'egrp', [(i + 1, i) for i in range(groups - 1)])  3.74 us
    unnamed x16, local copies, waits for them, and re-layouts  2.92 us
    pallas_call x1, Pallas kernels, prepared(): pl.pallas_call(prepare_kernel, name='prepare', out_shape=[jax.ShapeDtypeS...  2.71 us
  transfers between devices with their start and end apart: 8, of which 6 were waited for; matrix products, arithmetic and copies ran while one was open for 0% of the time, Pallas kernels for 6%

profile of v1, /device:TPU:4, one launch (start us, length us, event | category | flops | bytes accessed | tf_op | source)
XLA Modules:
  0.0 46.9 jit_solution(2030931809041022750)
XLA Ops:
  0.0 1.3 %copy.7.refs_0_ = s32[16,2]{1,0:T(8,128)} copy(s32[16,2]{0,1:T(2,128)} %param.8) | data formatting | bytes 256 | tf_op args[2]
  1.3 4.4 %lesser.1 = (bf16[4,64,128]{2,1,0:T(8,128)(2,1)}, bf16[4,64,128]{2,1,0:T(8,128)(2,1)}, bf16[4,64,128]{2,1,0:T(8,128)(2,1)}, bf16[4,64,128]{2,1,0:T(8,128)(2,1)}) custom-call(s32[16,2]{1,0:T(8,128)} %copy.7.refs_0_, bf16[1,16,3,64,128]{4,3,2,1,0:T(8,128)(2,1)} %refs_1_.1, bf16[1,16,64,128]{3,2,1,0:T(8,128)(2,1)} %refs_2_.1), custom_call_target="tpu_custom_call" | custom-call | flops 400000000 | bytes 2000000 | tf_op jit(solution)/shard_map/lesser/pallas_call | solution.py:68
  5.8 1.6 %collective-permute-start = (bf16[4,64,128]{2,1,0:T(8,128)(2,1)}, bf16[4,64,128]{2,1,0:T(8,128)(2,1)S(1)}, u32[]{:S(2)}, u32[]{:S(2)}) collective-permute-start(bf16[4,64,128]{2,1,0:T(8,128)(2,1)} %get-tuple-element.16), channel_id=1, source_target_pairs={{0,1},{1,0},{2,3},{3,2},{4,5},{5,4},{6,7},{7,6},{8,9},{9,8},{10,11... | collective-permute-start | bytes 196616 | tf_op jit(solution)/shard_map/ppermute | solution.py:186
  7.4 2.6 %collective-permute-start.1 = (bf16[4,64,128]{2,1,0:T(8,128)(2,1)}, bf16[4,64,128]{2,1,0:T(8,128)(2,1)S(1)}, u32[]{:S(2)}, u32[]{:S(2)}) collective-permute-start(bf16[4,64,128]{2,1,0:T(8,128)(2,1)} %get-tuple-element.17), channel_id=1, source_target_pairs={{0,2},{1,3},{2,0},{3,1},{4,6},{5,7},{6,4},{7,5},{8,10},{9,11},{10,... | collective-permute-start | bytes 196616 | tf_op jit(solution)/shard_map/ppermute | solution.py:186
  10.0 0.2 collective-permute-start.2
  10.2 0.1 collective-permute-done
  10.3 4.6 %collective-permute-done.1 = bf16[4,64,128]{2,1,0:T(8,128)(2,1)S(1)} collective-permute-done((bf16[4,64,128]{2,1,0:T(8,128)(2,1)}, bf16[4,64,128]{2,1,0:T(8,128)(2,1)S(1)}, u32[]{:S(2)}, u32[]{:S(2)}) %collective-permute-start.1) | collective-permute-done | bytes 65568 | tf_op jit(solution)/shard_map/ppermute | solution.py:186
  14.8 1.4 %collective-permute-done.2 = bf16[4,64,128]{2,1,0:T(8,128)(2,1)S(1)} collective-permute-done((bf16[4,64,128]{2,1,0:T(8,128)(2,1)}, bf16[4,64,128]{2,1,0:T(8,128)(2,1)S(1)}, u32[]{:S(2)}, u32[]{:S(2)}) %collective-permute-start.2) | collective-permute-done | bytes 65568 | tf_op jit(solution)/shard_map/ppermute | solution.py:186
  16.2 0.9 %pad_maximum_fusion = bf16[4,4,64,128]{3,2,1,0:T(8,128)(2,1)S(1)} fusion(bf16[1,4,64,128]{3,2,1,0:T(8,128)(2,1)S(1)} %bitcast.11, bf16[1,4,64,128]{3,2,1,0:T(8,128)(2,1)S(1)} %bitcast.10, bf16[1,4,64,128]{3,2,1,0:T(8,128)(2,1)S(1)} %bitcast.9, bf16[1,4,64,128]{3,2,1,0:T(8,128)(2,1)} %bitcast.8), kind=kLoop, calls=%fused_computation | loop fusion | flops 393216 | bytes 524288 | tf_op jit(solution)/shard_map/stack | solution.py:196
  17.1 1.9 %collective-permute-start.3 = (bf16[4,4,64,128]{3,2,1,0:T(8,128)(2,1)S(1)}, bf16[4,4,64,128]{3,2,1,0:T(8,128)(2,1)S(1)}, u32[]{:S(2)}, u32[]{:S(2)}) collective-permute-start(bf16[4,4,64,128]{3,2,1,0:T(8,128)(2,1)S(1)} %pad_maximum_fusion), channel_id=1, source_target_pairs={{0,4},{4,8},{8,12},{12,16},{16,20},{20,24},{24,28},{1,5},{5,9},{9,... | collective-permute-start | bytes 786440 | tf_op jit(solution)/shard_map/ppermute | solution.py:197
  19.1 2.7 %prepare.1 = (bf16[4,6,128,256]{3,2,1,0:T(8,128)(2,1)}, bf16[4,128,384]{2,1,0:T(8,128)(2,1)}) custom-call(f32[6]{0:T(128)} %occupancy.1, bf16[6,4,64,128]{3,2,1,0:T(8,128)(2,1)} %couplings.1), custom_call_target="tpu_custom_call" | custom-call | flops 200000000 | bytes 2000000 | tf_op jit(solution)/shard_map/prepare/pallas_call | solution.py:93
  21.8 4.5 %collective-permute-start.4 = (bf16[4,4,64,128]{3,2,1,0:T(8,128)(2,1)S(1)}, bf16[4,4,64,128]{3,2,1,0:T(8,128)(2,1)S(1)}, u32[]{:S(2)}, u32[]{:S(2)}) collective-permute-start(bf16[4,4,64,128]{3,2,1,0:T(8,128)(2,1)S(1)} %pad_maximum_fusion), channel_id=1, source_target_pairs={{4,0},{8,4},{12,8},{16,12},{20,16},{24,20},{28,24},{5,1},{9,5},{13... | collective-permute-start | bytes 786440 | tf_op jit(solution)/shard_map/ppermute | solution.py:198
  26.3 0.0 collective-permute-done.3
  26.4 3.7 %collective-permute-done.4 = bf16[4,4,64,128]{3,2,1,0:T(8,128)(2,1)S(1)} collective-permute-done((bf16[4,4,64,128]{3,2,1,0:T(8,128)(2,1)S(1)}, bf16[4,4,64,128]{3,2,1,0:T(8,128)(2,1)S(1)}, u32[]{:S(2)}, u32[]{:S(2)}) %collective-permute-start.4) | collective-permute-done | bytes 262176 | tf_op jit(solution)/shard_map/ppermute | solution.py:198
  30.2 0.9 %copy-done = bf16[12,4,64,128]{3,2,1,0:T(8,128)(2,1)} copy-done((bf16[12,4,64,128]{3,2,1,0:T(8,128)(2,1)}, bf16[12,4,64,128]{3,2,1,0:T(8,128)(2,1)S(1)}, u32[]{:S(2)}) %copy-start) | copy-done | bytes 786456
  31.1 4.5 %modes.1 = (bf16[4,64,128]{2,1,0:T(8,128)(2,1)}, bf16[4,64,128]{2,1,0:T(8,128)(2,1)}, bf16[4,64,128]{2,1,0:T(8,128)(2,1)}, bf16[4,64,128]{2,1,0:T(8,128)(2,1)}) custom-call(s32[6]{0:T(128)} %shifts.1, bf16[12,4,64,128]{3,2,1,0:T(8,128)(2,1)} %copy-done, bf16[4,6,128,256]{3,2,1,0:T(8,128)(2,1)} %get-tuple-element.19.right, ...), custom_call_target="tpu_custom_call" | custom-call | flops 400000000 | bytes 2000000 | tf_op jit(solution)/shard_map/modes/pallas_call | solution.py:150
  35.6 0.0 collective-permute-start.5
  35.6 2.3 %collective-permute-start.6 = (bf16[4,64,128]{2,1,0:T(8,128)(2,1)}, bf16[4,64,128]{2,1,0:T(8,128)(2,1)S(1)}, u32[]{:S(2)}, u32[]{:S(2)}) collective-permute-start(bf16[4,64,128]{2,1,0:T(8,128)(2,1)} %get-tuple-element.23), channel_id=1, source_target_pairs={{0,2},{1,3},{2,0},{3,1},{4,6},{5,7},{6,4},{7,5},{8,10},{9,11},{10,... | collective-permute-start | bytes 196616 | tf_op jit(solution)/shard_map/ppermute | solution.py:186
  38.0 2.0 %collective-permute-start.7 = (bf16[4,64,128]{2,1,0:T(8,128)(2,1)}, bf16[4,64,128]{2,1,0:T(8,128)(2,1)S(1)}, u32[]{:S(2)}, u32[]{:S(2)}) collective-permute-start(bf16[4,64,128]{2,1,0:T(8,128)(2,1)} %get-tuple-element.24), channel_id=1, source_target_pairs={{0,3},{1,2},{2,1},{3,0},{4,7},{5,6},{6,5},{7,4},{8,11},{9,10},{10,... | collective-permute-start | bytes 196616 | tf_op jit(solution)/shard_map/ppermute | solution.py:186
  40.0 2.1 %collective-permute-done.5.refs_1_ = bf16[4,64,128]{2,1,0:T(8,128)(2,1)S(1)} collective-permute-done((bf16[4,64,128]{2,1,0:T(8,128)(2,1)}, bf16[4,64,128]{2,1,0:T(8,128)(2,1)S(1)}, u32[]{:S(2)}, u32[]{:S(2)}) %collective-permute-start.5) | collective-permute-done | bytes 65568 | tf_op jit(solution)/shard_map/ppermute | solution.py:186
  42.1 0.0 collective-permute-done.6.refs_2_
  42.1 2.5 %collective-permute-done.7.refs_3_ = bf16[4,64,128]{2,1,0:T(8,128)(2,1)S(1)} collective-permute-done((bf16[4,64,128]{2,1,0:T(8,128)(2,1)}, bf16[4,64,128]{2,1,0:T(8,128)(2,1)S(1)}, u32[]{:S(2)}, u32[]{:S(2)}) %collective-permute-start.7) | collective-permute-done | bytes 65568 | tf_op jit(solution)/shard_map/ppermute | solution.py:186
  44.6 0.6 %copy-done.4 = bf16[4,64,128]{2,1,0:T(8,128)(2,1)} copy-done((bf16[4,64,128]{2,1,0:T(8,128)(2,1)}, bf16[4,64,128]{2,1,0:T(8,128)(2,1)S(1)}, u32[]{:S(2)}) %copy-start.4) | copy-done | bytes 65560
  45.2 1.7 %join.1 = bf16[1,16,64,128]{3,2,1,0:T(8,128)(2,1)} custom-call(bf16[4,64,128]{2,1,0:T(8,128)(2,1)} %get-tuple-element.21.refs_0_, bf16[4,64,128]{2,1,0:T(8,128)(2,1)} %copy-done.2, bf16[4,64,128]{2,1,0:T(8,128)(2,1)} %copy-done.3, bf16[4,64,128]{2,1,0:T(8,128)(2,1)} %copy-done.4), custom_call_target="tpu_custom_call" | custom-call | tf_op jit(solution)/shard_map/join/pallas_call | solution.py:175
  (14 shorter events, 0.1 us)
Async XLA Ops:
  5.8 20.5 %copy-start.1 = (bf16[4,64,128]{2,1,0:T(8,128)(2,1)S(1)}, bf16[4,64,128]{2,1,0:T(8,128)(2,1)}, u32[]{:S(2)}) copy-start(bf16[4,64,128]{2,1,0:T(8,128)(2,1)} %get-tuple-element.15) | copy-start | bytes 196612
  5.8 4.5 %collective-permute-start = (bf16[4,64,128]{2,1,0:T(8,128)(2,1)}, bf16[4,64,128]{2,1,0:T(8,128)(2,1)S(1)}, u32[]{:S(2)}, u32[]{:S(2)}) collective-permute-start(bf16[4,64,128]{2,1,0:T(8,128)(2,1)} %get-tuple-element.16), channel_id=1, source_target_pairs={{0,1},{1,0},{2,3},{3,2},{4,5},{5,4},{6,7},{7,6},{8,9},{9,8},{10,11... | collective-permute-start | bytes 196616 | tf_op jit(solution)/shard_map/ppermute | solution.py:186
  7.4 7.5 %collective-permute-start.1 = (bf16[4,64,128]{2,1,0:T(8,128)(2,1)}, bf16[4,64,128]{2,1,0:T(8,128)(2,1)S(1)}, u32[]{:S(2)}, u32[]{:S(2)}) collective-permute-start(bf16[4,64,128]{2,1,0:T(8,128)(2,1)} %get-tuple-element.17), channel_id=1, source_target_pairs={{0,2},{1,3},{2,0},{3,1},{4,6},{5,7},{6,4},{7,5},{8,10},{9,11},{10,... | collective-permute-start | bytes 196616 | tf_op jit(solution)/shard_map/ppermute | solution.py:186
  10.0 6.3 %collective-permute-start.2 = (bf16[4,64,128]{2,1,0:T(8,128)(2,1)}, bf16[4,64,128]{2,1,0:T(8,128)(2,1)S(1)}, u32[]{:S(2)}, u32[]{:S(2)}) collective-permute-start(bf16[4,64,128]{2,1,0:T(8,128)(2,1)} %get-tuple-element.18), channel_id=1, source_target_pairs={{0,3},{1,2},{2,1},{3,0},{4,7},{5,6},{6,5},{7,4},{8,11},{9,10},{10,... | collective-permute-start | bytes 196616 | tf_op jit(solution)/shard_map/ppermute | solution.py:186
  17.1 9.2 %collective-permute-start.3 = (bf16[4,4,64,128]{3,2,1,0:T(8,128)(2,1)S(1)}, bf16[4,4,64,128]{3,2,1,0:T(8,128)(2,1)S(1)}, u32[]{:S(2)}, u32[]{:S(2)}) collective-permute-start(bf16[4,4,64,128]{3,2,1,0:T(8,128)(2,1)S(1)} %pad_maximum_fusion), channel_id=1, source_target_pairs={{0,4},{4,8},{8,12},{12,16},{16,20},{20,24},{24,28},{1,5},{5,9},{9,... | collective-permute-start | bytes 786440 | tf_op jit(solution)/shard_map/ppermute | solution.py:197
  21.8 8.4 %collective-permute-start.4 = (bf16[4,4,64,128]{3,2,1,0:T(8,128)(2,1)S(1)}, bf16[4,4,64,128]{3,2,1,0:T(8,128)(2,1)S(1)}, u32[]{:S(2)}, u32[]{:S(2)}) collective-permute-start(bf16[4,4,64,128]{3,2,1,0:T(8,128)(2,1)S(1)} %pad_maximum_fusion), channel_id=1, source_target_pairs={{4,0},{8,4},{12,8},{16,12},{20,16},{24,20},{28,24},{5,1},{9,5},{13... | collective-permute-start | bytes 786440 | tf_op jit(solution)/shard_map/ppermute | solution.py:198
  30.2 0.9 %copy-start = (bf16[12,4,64,128]{3,2,1,0:T(8,128)(2,1)}, bf16[12,4,64,128]{3,2,1,0:T(8,128)(2,1)S(1)}, u32[]{:S(2)}) copy-start(bf16[12,4,64,128]{3,2,1,0:T(8,128)(2,1)S(1)} %constant_dynamic-update-slice_fusion.here) | copy-start | bytes 2359300
  35.6 6.5 %collective-permute-start.5 = (bf16[4,64,128]{2,1,0:T(8,128)(2,1)}, bf16[4,64,128]{2,1,0:T(8,128)(2,1)S(1)}, u32[]{:S(2)}, u32[]{:S(2)}) collective-permute-start(bf16[4,64,128]{2,1,0:T(8,128)(2,1)} %get-tuple-element.22), channel_id=1, source_target_pairs={{0,1},{1,0},{2,3},{3,2},{4,5},{5,4},{6,7},{7,6},{8,9},{9,8},{10,11... | collective-permute-start | bytes 196616 | tf_op jit(solution)/shard_map/ppermute | solution.py:186
  35.6 6.5 %collective-permute-start.6 = (bf16[4,64,128]{2,1,0:T(8,128)(2,1)}, bf16[4,64,128]{2,1,0:T(8,128)(2,1)S(1)}, u32[]{:S(2)}, u32[]{:S(2)}) collective-permute-start(bf16[4,64,128]{2,1,0:T(8,128)(2,1)} %get-tuple-element.23), channel_id=1, source_target_pairs={{0,2},{1,3},{2,0},{3,1},{4,6},{5,7},{6,4},{7,5},{8,10},{9,11},{10,... | collective-permute-start | bytes 196616 | tf_op jit(solution)/shard_map/ppermute | solution.py:186
  38.0 6.7 %collective-permute-start.7 = (bf16[4,64,128]{2,1,0:T(8,128)(2,1)}, bf16[4,64,128]{2,1,0:T(8,128)(2,1)S(1)}, u32[]{:S(2)}, u32[]{:S(2)}) collective-permute-start(bf16[4,64,128]{2,1,0:T(8,128)(2,1)} %get-tuple-element.24), channel_id=1, source_target_pairs={{0,3},{1,2},{2,1},{3,0},{4,7},{5,6},{6,5},{7,4},{8,11},{9,10},{10,... | collective-permute-start | bytes 196616 | tf_op jit(solution)/shard_map/ppermute | solution.py:186
  42.1 2.5 %copy-start.2 = (bf16[4,64,128]{2,1,0:T(8,128)(2,1)}, bf16[4,64,128]{2,1,0:T(8,128)(2,1)S(1)}, u32[]{:S(2)}) copy-start(bf16[4,64,128]{2,1,0:T(8,128)(2,1)S(1)} %collective-permute-done.5.refs_1_) | copy-start | bytes 196612
  42.1 2.5 %copy-start.3 = (bf16[4,64,128]{2,1,0:T(8,128)(2,1)}, bf16[4,64,128]{2,1,0:T(8,128)(2,1)S(1)}, u32[]{:S(2)}) copy-start(bf16[4,64,128]{2,1,0:T(8,128)(2,1)S(1)} %collective-permute-done.6.refs_2_) | copy-start | bytes 196612
  44.6 0.6 %copy-start.4 = (bf16[4,64,128]{2,1,0:T(8,128)(2,1)}, bf16[4,64,128]{2,1,0:T(8,128)(2,1)S(1)}, u32[]{:S(2)}) copy-start(bf16[4,64,128]{2,1,0:T(8,128)(2,1)S(1)} %collective-permute-done.7.refs_3_) | copy-start | bytes 196612

commit v2 on v0

v2 whole, which is shorter than its diff:
```python
import jax
import jax.numpy as jnp
from jax import lax
from jax.experimental import pallas as pl
from jax.experimental.pallas import tpu as pltpu
from jax.sharding import PartitionSpec as P


VMEM = pl.BlockSpec(memory_space=pltpu.VMEM)
SMEM = pl.BlockSpec(memory_space=pltpu.SMEM)
HBM = pl.BlockSpec(memory_space=pltpu.HBM)
BF16 = jnp.bfloat16
F32 = jnp.float32
NT = (((1,), (1,)), ((), ()))


def limited():
    return pltpu.CompilerParams(vmem_limit_bytes=12 * 1024 * 1024)


def cost(flops):
    return pl.CostEstimate(flops=flops, bytes_accessed=1_000_000, transcendentals=0)


def two_power(n):
    return n & (n - 1) == 0


def partner(i, k, n):
    return i ^ k if two_power(n) else (i + k) % n


def target_at(me, k, n):
    return me ^ k if two_power(n) else lax.rem(me + k, n)


def source_at(me, k, n):
    return me ^ k if two_power(n) else lax.rem(me + n - k, n)


def place_of(me, t, n):
    if two_power(n):
        return (t & ~(n - 1)) + (me ^ (t & (n - 1)))
    inside = lax.rem(t, n)
    return t - inside + lax.rem(me - inside + n, n)


def turned(block):
    half = block.shape[-1] // 2
    return jnp.concatenate([-block[:, half:], block[:, :half]], -1)


def widened(block):
    return jnp.concatenate([block, turned(block)], 0)


def lesser_of(blocks, chosen):
    total = None
    for block, other in zip(blocks, chosen):
        half = jnp.dot(block, widened(other), preferred_element_type=F32).astype(BF16)
        term = lax.dot_general(half, widened(block), NT, preferred_element_type=F32)
        total = term if total is None else total + term
    return total.astype(BF16)


def opened():
    def kernel(out):
        out[...] = jnp.zeros_like(out)

    return pl.pallas_call(
        kernel,
        name="opening",
        out_shape=jax.ShapeDtypeStruct((8, 128), jnp.int32),
        out_specs=VMEM,
        compiler_params=limited(),
        cost_estimate=cost(4_000_000_000),
    )()


def lesser_blocks(n, per, opening, neighbours, green, sigma):
    _, _, terms, orb, wide = green.shape

    def kernel(opening, neighbours, green, sigma, *outs):
        me = lax.axis_index("eloc")
        for k in range(n - 1, -1, -1):
            for i in range(per):
                atom = target_at(me, k, n) * per + i
                chosen = [sigma[0, atom]] + [sigma[0, neighbours[j, atom]] for j in range(terms - 1)]
                outs[k][i] = lesser_of([green[0, atom, j] for j in range(terms)], chosen)

    return pl.pallas_call(
        kernel,
        name="lesser",
        out_shape=[jax.ShapeDtypeStruct((per, orb, wide), BF16) for _ in range(n)],
        in_specs=[VMEM, SMEM, VMEM, VMEM],
        out_specs=[VMEM for _ in range(n)],
        compiler_params=limited(),
        cost_estimate=cost(400_000_000),
    )(opening, neighbours, green, sigma)


def prepared(occupancy, couplings):
    modes, per, orb, wide = couplings.shape

    def kernel(occupancy, couplings, right, left):
        for a in range(per):
            for m in range(modes):
                block = couplings[m, a]
                across = widened(block.astype(F32)).T
                occ = occupancy[m]
                right[a, m, :wide] = (across * (occ + 1.0)).astype(BF16)
                right[a, m, wide:] = (across * occ).astype(BF16)
            left[a, :orb] = jnp.concatenate([couplings[m, a][:, :orb] for m in range(modes)], 1)
            left[a, orb:] = jnp.concatenate([couplings[m, a][:, orb:] for m in range(modes)], 1)

    return pl.pallas_call(
        kernel,
        name="prepare",
        out_shape=[
            jax.ShapeDtypeStruct((per, modes, 2 * wide, wide), BF16),
            jax.ShapeDtypeStruct((per, 2 * orb, modes * orb), BF16),
        ],
        in_specs=[SMEM, VMEM],
        out_specs=[VMEM, VMEM],
        compiler_params=limited(),
        cost_estimate=cost(200_000_000),
    )(occupancy, couplings)


def mode_blocks(n, ks, shifts, extended, right, left):
    per, modes, _, wide = right.shape
    orb = wide // 2
    width = 2 if len(ks) % 2 == 0 else 1

    def kernel(shifts, extended, right, left, *rest):
        outs, stack = rest[: len(ks)], rest[-1]
        me = lax.axis_index("eloc")
        even = lax.axis_index("egrp") & 1 == 0
        places = {}
        for m in range(modes):
            for k in ks:
                e = target_at(me, k, n) + n
                above, below = place_of(me, e + shifts[m], n), place_of(me, e - shifts[m], n)
                above = jnp.where(even & (above >= 2 * n), above - 2 * n, above)
                below = jnp.where(even & (below < n), below + 2 * n, below)
                places[m, k] = (above, below)
        for a in range(per):
            for m in range(modes):
                rows = []
                for k in ks:
                    above, below = places[m, k]
                    rows.append(jnp.concatenate([extended[above, a], extended[below, a]], 1))
                stacked = jnp.concatenate(rows, 0)
                product = jnp.dot(stacked, right[a, m], preferred_element_type=F32).astype(BF16)
                for q in range(len(ks)):
                    p, w = divmod(q, width)
                    stack[a, p, m * orb : (m + 1) * orb, w * wide : (w + 1) * wide] = (
                        product[q * orb : (q + 1) * orb]
                    )
            for p in range(len(ks) // width):
                both = jnp.dot(left[a], stack[a, p], preferred_element_type=F32)
                for w in range(width):
                    piece = both[:, w * wide : (w + 1) * wide]
                    outs[p * width + w][a] = (piece[:orb] + turned(piece[orb:])).astype(BF16)

    return pl.pallas_call(
        kernel,
        out_shape=[jax.ShapeDtypeStruct((per, orb, wide), BF16) for _ in ks],
        in_specs=[SMEM, VMEM, VMEM, VMEM],
        out_specs=[VMEM for _ in ks],
        scratch_shapes=[pltpu.VMEM((per, len(ks) // width, modes * orb, width * wide), BF16)],
        compiler_params=limited(),
        cost_estimate=cost(400_000_000),
    )(shifts, extended, right, left)


def joined(n, blocks):
    per, orb, wide = blocks[0].shape

    def kernel(*refs):
        blocks, out, done = refs[:n], refs[n], refs[n + 1]
        me = lax.axis_index("eloc")
        copies = []
        for k in range(n):
            place = out.at[0, pl.ds(source_at(me, k, n) * per, per)]
            copies.append(pltpu.make_async_copy(blocks[k], place, done.at[k]))
        for copy in copies:
            copy.start()
        for copy in copies:
            copy.wait()

    return pl.pallas_call(
        kernel,
        name="join",
        out_shape=jax.ShapeDtypeStruct((1, n * per, orb, wide), BF16),
        in_specs=[VMEM for _ in blocks],
        out_specs=HBM,
        scratch_shapes=[pltpu.SemaphoreType.DMA((n,))],
        compiler_params=limited(),
    )(*blocks)


def swapped(n, k, block):
    return lax.ppermute(block, "eloc", [(i, partner(i, k, n)) for i in range(n)])


def traded(groups, first, block):
    pairs = []
    for i in range(first, groups - 1, 2):
        pairs += [(i, i + 1), (i + 1, i)]
    return lax.ppermute(block, "egrp", pairs)


def shards(green_blocks, sigma_prev, neighbours, couplings, occupancy, shifts):
    n, groups = lax.axis_size("eloc"), lax.axis_size("egrp")
    per = couplings.shape[1]
    made = lesser_blocks(n, per, opened(), neighbours.T, green_blocks, sigma_prev)
    held = [made[0]] + [swapped(n, k, made[k]) for k in range(1, n)]
    right, left = prepared(occupancy, couplings)
    here = jnp.stack(held)
    here, right, left = lax.optimization_barrier((here, right, left))
    outer = traded(groups, 1, here)
    inner = traded(groups, 0, here)
    extended = jnp.concatenate([inner, here, outer], 0)
    order = list(range(n - 1, -1, -1))
    made = mode_blocks(n, order, shifts, extended, right, left)[::-1]
    back = [made[0]] + [swapped(n, k, made[k]) for k in range(1, n)]
    return joined(n, back)


def solution(mesh):
    return jax.shard_map(
        shards,
        mesh=mesh,
        in_specs=(
            P(("egrp", "eloc"), None, None, None, None),
            P(("egrp", "eloc"), None, None, None),
            P(),
            P(None, "eloc", None, None),
            P(),
            P(),
        ),
        out_specs=P(("egrp", "eloc"), None, None, None),
        check_vma=False,
    )
```

time: 81.2 us -> 37 us (0.46)
  between operations: 19.6 us -> 0.1 us
  blocking collectives: 14.7 us -> 0 us
  matrix products: 12.2 us -> 0 us
  waiting for transfers between devices: 5.2 us -> 15.3 us
  other arithmetic: 8.64 us -> 0.12 us
  Pallas kernels: 0 us -> 7.58 us
  local copies, waits for them, and re-layouts: 8.7 us -> 1.22 us
  starting transfers between devices: 11.5 us -> 12.5 us
    all_to_all x1 -> x0, blocking collectives: 14.7 us -> none  [shards(): lax.all_to_all(result, 'eloc', split_axis=0, concat_axis=1, tiled=True)]
    dot_general x13 -> x0, matrix products: 12.2 us -> none  [the longest x1 5.04 us: shards(): jnp.einsum('akij,akjl->ail', half_product, adjoint_form(blocks), preferre...]
    ppermute x2 -> x8, waiting for transfers between devices: 5.2 us -> 15.3 us  [the longest x6 8.4 us: swapped(): lax.ppermute(block, 'eloc', [(i, partner(i, k, n)) for i in range(n)])]
    pallas_call x0 -> x5, Pallas kernels: none -> 7.58 us  [the longest x1 2.96 us: lesser_blocks(): pl.pallas_call(kernel, name='lesser', out_shape=[jax.ShapeDtypeStruct((pe...]
    ppermute x2 -> x8, starting transfers between devices: 6.63 us -> 12.5 us  [the longest x6 8.9 us: swapped(): lax.ppermute(block, 'eloc', [(i, partner(i, k, n)) for i in range(n)])]
    all_to_all x1 -> x0, starting transfers between devices: 4.86 us -> none  [shards(): lax.all_to_all(lesser[None], 'eloc', split_axis=1, concat_axis=0, tiled=T...]
    add x2 -> x0, other arithmetic: 4.77 us -> none  [shards(): (occupancy[mode_index] + 1.0) * upper_part]
    neg x8 -> x0, other arithmetic: 3.05 us -> none  [the longest x7 2.98 us: widened_form(): lower_rows = jnp.concatenate([-imag_part, real_part], -1)]
  transfers between devices with their start and end apart: 3 -> 8, of which waited for: 1 -> 5; matrix products, arithmetic and copies ran while one was open for 5% -> 0% of each run, Pallas kernels for 0% -> 4%
where the time goes in v2:
time: 37 us; the launch traced here: 36.8 us
  waiting for transfers between devices  15.3 us (41%)
  starting transfers between devices  12.5 us (34%)
  Pallas kernels  7.58 us (20%)
  local copies, waits for them, and re-layouts  1.22 us (3%)
    ppermute x6, starting transfers between devices, swapped(): lax.ppermute(block, 'eloc', [(i, partner(i, k, n)) for i in range(n)])  8.9 us
    ppermute x6, waiting for transfers between devices, swapped(): lax.ppermute(block, 'eloc', [(i, partner(i, k, n)) for i in range(n)])  8.4 us
    ppermute x2, waiting for transfers between devices, traded(): return lax.ppermute(block, 'egrp', pairs)  6.91 us
    ppermute x2, starting transfers between devices, traded(): return lax.ppermute(block, 'egrp', pairs)  3.58 us
    pallas_call x1, Pallas kernels, lesser_blocks(): pl.pallas_call(kernel, name='lesser', out_shape=[jax.ShapeDtypeStruct((pe...  2.96 us
    pallas_call x1, Pallas kernels, mode_blocks(): pl.pallas_call(kernel, out_shape=[jax.ShapeDtypeStruct((per, orb, wide),...  2.44 us
    pallas_call x1, Pallas kernels, prepared(): pl.pallas_call(kernel, name='prepare', out_shape=[jax.ShapeDtypeStruct((p...  1.45 us
    unnamed x12, local copies, waits for them, and re-layouts  1.22 us
  transfers between devices with their start and end apart: 8, of which 5 were waited for; matrix products, arithmetic and copies ran while one was open for 0% of the time, Pallas kernels for 4%

profile of v2, /device:TPU:4, one launch (start us, length us, event | category | flops | bytes accessed | tf_op | source)
XLA Modules:
  0.0 36.8 jit_solution(10936244093854099495)
XLA Ops:
  0.0 0.6 %copy-done.4 = s32[16,2]{0,1:T(2,128)S(1)} copy-done((s32[16,2]{0,1:T(2,128)S(1)}, s32[16,2]{0,1:T(2,128)}, u32[]{:S(2)}) %copy-start.4) | copy-done | bytes 152
  0.7 0.3 copy-done.3
  1.0 0.3 copy-done.1
  1.2 3.0 %lesser.1 = (bf16[4,64,128]{2,1,0:T(8,128)(2,1)S(1)}, bf16[4,64,128]{2,1,0:T(8,128)(2,1)S(1)}, bf16[4,64,128]{2,1,0:T(8,128)(2,1)S(1)}, bf16[4,64,128]{2,1,0:T(8,128)(2,1)S(1)}) custom-call(s32[8,128]{1,0:T(8,128)S(1)} %opening.1, s32[2,16]{1,0:T(2,128)S(1)} %bitcast.6, bf16[1,16,3,64,128]{4,3,2,1,0:T(8,128)(2,1)S(1)} %copy-done.1, ...), custom_call_target="tpu_custom_call" | custom-call | flops 400000000 | bytes 1000000 | tf_op jit(solution)/shard_map/lesser/pallas_call | solution.py:91
  4.2 0.0 copy-start
  4.2 1.6 %collective-permute-start = (bf16[4,64,128]{2,1,0:T(8,128)(2,1)S(1)}, bf16[4,64,128]{2,1,0:T(8,128)(2,1)S(1)}, u32[]{:S(2)}, u32[]{:S(2)}) collective-permute-start(bf16[4,64,128]{2,1,0:T(8,128)(2,1)S(1)} %get-tuple-element.19), channel_id=1, source_target_pairs={{0,1},{1,0},{2,3},{3,2},{4,5},{5,4},{6,7},{7,6},{8,9},{9,8},{10,11... | collective-permute-start | bytes 196616 | tf_op jit(solution)/shard_map/ppermute | solution.py:204
  5.9 2.6 %collective-permute-start.1 = (bf16[4,64,128]{2,1,0:T(8,128)(2,1)S(1)}, bf16[4,64,128]{2,1,0:T(8,128)(2,1)S(1)}, u32[]{:S(2)}, u32[]{:S(2)}) collective-permute-start(bf16[4,64,128]{2,1,0:T(8,128)(2,1)S(1)} %get-tuple-element.20), channel_id=1, source_target_pairs={{0,2},{1,3},{2,0},{3,1},{4,6},{5,7},{6,4},{7,5},{8,10},{9,11},{10,... | collective-permute-start | bytes 196616 | tf_op jit(solution)/shard_map/ppermute | solution.py:204
  8.4 0.2 collective-permute-start.2
  8.7 1.4 %prepare.1 = (bf16[4,6,256,128]{3,2,1,0:T(8,128)(2,1)S(1)}, bf16[4,128,384]{2,1,0:T(8,128)(2,1)S(1)}) custom-call(f32[6]{0:T(128)S(1)} %copy-done.5, bf16[6,4,64,128]{3,2,1,0:T(8,128)(2,1)S(1)} %copy-done.2), custom_call_target="tpu_custom_call" | custom-call | flops 200000000 | bytes 1000000 | tf_op jit(solution)/shard_map/prepare/pallas_call | solution.py:116
  10.1 0.0 collective-permute-done
  10.1 3.0 %collective-permute-done.1 = bf16[4,64,128]{2,1,0:T(8,128)(2,1)S(1)} collective-permute-done((bf16[4,64,128]{2,1,0:T(8,128)(2,1)S(1)}, bf16[4,64,128]{2,1,0:T(8,128)(2,1)S(1)}, u32[]{:S(2)}, u32[]{:S(2)}) %collective-permute-start.1) | collective-permute-done | bytes 65568 | tf_op jit(solution)/shard_map/ppermute | solution.py:204
  13.1 1.4 %collective-permute-done.2 = bf16[4,64,128]{2,1,0:T(8,128)(2,1)S(1)} collective-permute-done((bf16[4,64,128]{2,1,0:T(8,128)(2,1)S(1)}, bf16[4,64,128]{2,1,0:T(8,128)(2,1)S(1)}, u32[]{:S(2)}, u32[]{:S(2)}) %collective-permute-start.2) | collective-permute-done | bytes 65568 | tf_op jit(solution)/shard_map/ppermute | solution.py:204
  14.6 1.9 %collective-permute-start.4 = (bf16[4,4,64,128]{3,2,1,0:T(8,128)(2,1)S(1)}, bf16[4,4,64,128]{3,2,1,0:T(8,128)(2,1)S(1)}, u32[]{:S(2)}, u32[]{:S(2)}) collective-permute-start(bf16[4,4,64,128]{3,2,1,0:T(8,128)(2,1)S(1)} %pad_maximum_fusion.1), channel_id=1, source_target_pairs={{4,8},{8,4},{12,16},{16,12},{20,24},{24,20},{5,9},{9,5},{13,17},{1... | collective-permute-start | bytes 786440 | tf_op jit(solution)/shard_map/ppermute | solution.py:211
  16.5 1.7 %collective-permute-start.3 = (bf16[4,4,64,128]{3,2,1,0:T(8,128)(2,1)S(1)}, bf16[4,4,64,128]{3,2,1,0:T(8,128)(2,1)S(1)}, u32[]{:S(2)}, u32[]{:S(2)}) collective-permute-start(bf16[4,4,64,128]{3,2,1,0:T(8,128)(2,1)S(1)} %pad_maximum_fusion.1), channel_id=1, source_target_pairs={{0,4},{4,0},{8,12},{12,8},{16,20},{20,16},{24,28},{28,24},{1,5},{5... | collective-permute-start | bytes 786440 | tf_op jit(solution)/shard_map/ppermute | solution.py:211
  18.1 6.9 %collective-permute-done.4 = bf16[4,4,64,128]{3,2,1,0:T(8,128)(2,1)S(1)} collective-permute-done((bf16[4,4,64,128]{3,2,1,0:T(8,128)(2,1)S(1)}, bf16[4,4,64,128]{3,2,1,0:T(8,128)(2,1)S(1)}, u32[]{:S(2)}, u32[]{:S(2)}) %collective-permute-start.4) | collective-permute-done | bytes 262176 | tf_op jit(solution)/shard_map/ppermute | solution.py:211
  25.1 0.0 collective-permute-done.3
  25.1 0.1 pad_maximum_fusion.extended
  25.2 2.4 %shard_map.64 = (bf16[4,64,128]{2,1,0:T(8,128)(2,1)S(1)}, bf16[4,64,128]{2,1,0:T(8,128)(2,1)S(1)}, bf16[4,64,128]{2,1,0:T(8,128)(2,1)S(1)}, bf16[4,64,128]{2,1,0:T(8,128)(2,1)S(1)}) custom-call(s32[6]{0:T(128)S(1)} %copy-done, bf16[12,4,64,128]{3,2,1,0:T(8,128)(2,1)S(1)} %pad_maximum_fusion.extended, bf16[4,6,256,128]{3,2,1,0:T(8,128)(2,1)S(1)} %get-tuple-element.25.right, ...), custom_call_target="tpu_custom_call" | custom-call | flops 400000000 | bytes 1000000 | tf_op jit(solution)/shard_map/pallas_call | solution.py:166
  27.6 0.1 collective-permute-start.5
  27.7 2.3 %collective-permute-start.6 = (bf16[4,64,128]{2,1,0:T(8,128)(2,1)S(1)}, bf16[4,64,128]{2,1,0:T(8,128)(2,1)S(1)}, u32[]{:S(2)}, u32[]{:S(2)}) collective-permute-start(bf16[4,64,128]{2,1,0:T(8,128)(2,1)S(1)} %get-tuple-element.29), channel_id=1, source_target_pairs={{0,2},{1,3},{2,0},{3,1},{4,6},{5,7},{6,4},{7,5},{8,10},{9,11},{10,... | collective-permute-start | bytes 196616 | tf_op jit(solution)/shard_map/ppermute | solution.py:204
  30.0 2.0 %collective-permute-start.7 = (bf16[4,64,128]{2,1,0:T(8,128)(2,1)S(1)}, bf16[4,64,128]{2,1,0:T(8,128)(2,1)S(1)}, u32[]{:S(2)}, u32[]{:S(2)}) collective-permute-start(bf16[4,64,128]{2,1,0:T(8,128)(2,1)S(1)} %get-tuple-element.30), channel_id=1, source_target_pairs={{0,3},{1,2},{2,1},{3,0},{4,7},{5,6},{6,5},{7,4},{8,11},{9,10},{10,... | collective-permute-start | bytes 196616 | tf_op jit(solution)/shard_map/ppermute | solution.py:204
  32.1 1.4 %collective-permute-done.6.refs_2_ = bf16[4,64,128]{2,1,0:T(8,128)(2,1)S(1)} collective-permute-done((bf16[4,64,128]{2,1,0:T(8,128)(2,1)S(1)}, bf16[4,64,128]{2,1,0:T(8,128)(2,1)S(1)}, u32[]{:S(2)}, u32[]{:S(2)}) %collective-permute-start.6) | collective-permute-done | bytes 65568 | tf_op jit(solution)/shard_map/ppermute | solution.py:204
  33.5 2.6 %collective-permute-done.7.refs_3_ = bf16[4,64,128]{2,1,0:T(8,128)(2,1)S(1)} collective-permute-done((bf16[4,64,128]{2,1,0:T(8,128)(2,1)S(1)}, bf16[4,64,128]{2,1,0:T(8,128)(2,1)S(1)}, u32[]{:S(2)}, u32[]{:S(2)}) %collective-permute-start.7) | collective-permute-done | bytes 65568 | tf_op jit(solution)/shard_map/ppermute | solution.py:204
  36.1 0.7 %join.1 = bf16[1,16,64,128]{3,2,1,0:T(8,128)(2,1)} custom-call(bf16[4,64,128]{2,1,0:T(8,128)(2,1)S(1)} %get-tuple-element.27.refs_0_, bf16[4,64,128]{2,1,0:T(8,128)(2,1)S(1)} %collective-permute-done.5.refs_1_, bf16[4,64,128]{2,1,0:T(8,128)(2,1)S(1)} %collective-permute-done.6.refs_2_, bf16[4,64,128]{2,1,0:T(8,128)(2,1)S(1)} %collective-permute-done.7.refs_3_), custom_call_target="tpu_custom_call" | custom-call | tf_op jit(solution)/shard_map/join/pallas_call | solution.py:192
  (11 shorter events, 0.1 us)
Async XLA Ops:
  0.0 0.7 %copy-start.4 = (s32[16,2]{0,1:T(2,128)S(1)}, s32[16,2]{0,1:T(2,128)}, u32[]{:S(2)}) copy-start(s32[16,2]{0,1:T(2,128)} %param.8) | copy-start | bytes 388
  0.0 1.0 %copy-start.3 = (bf16[1,16,64,128]{3,2,1,0:T(8,128)(2,1)S(1)}, bf16[1,16,64,128]{3,2,1,0:T(8,128)(2,1)}, u32[]{:S(2)}) copy-start(bf16[1,16,64,128]{3,2,1,0:T(8,128)(2,1)} %sigma.1) | copy-start | bytes 786436
  0.0 1.2 %copy-start.1 = (bf16[1,16,3,64,128]{4,3,2,1,0:T(8,128)(2,1)S(1)}, bf16[1,16,3,64,128]{4,3,2,1,0:T(8,128)(2,1)}, u32[]{:S(2)}) copy-start(bf16[1,16,3,64,128]{4,3,2,1,0:T(8,128)(2,1)} %green.1) | copy-start | bytes 2359300
  0.0 8.7 %copy-start.5 = (f32[6]{0:T(128)S(1)}, f32[6]{0:T(128)}, u32[]{:S(2)}) copy-start(f32[6]{0:T(128)} %occupancy.1) | copy-start | bytes 76
  0.0 8.7 %copy-start.2 = (bf16[6,4,64,128]{3,2,1,0:T(8,128)(2,1)S(1)}, bf16[6,4,64,128]{3,2,1,0:T(8,128)(2,1)}, u32[]{:S(2)}) copy-start(bf16[6,4,64,128]{3,2,1,0:T(8,128)(2,1)} %couplings.1) | copy-start | bytes 1179652
  4.2 21.0 %copy-start = (s32[6]{0:T(128)S(1)}, s32[6]{0:T(128)}, u32[]{:S(2)}) copy-start(s32[6]{0:T(128)} %shifts.1) | copy-start | bytes 76
  4.2 5.9 %collective-permute-start = (bf16[4,64,128]{2,1,0:T(8,128)(2,1)S(1)}, bf16[4,64,128]{2,1,0:T(8,128)(2,1)S(1)}, u32[]{:S(2)}, u32[]{:S(2)}) collective-permute-start(bf16[4,64,128]{2,1,0:T(8,128)(2,1)S(1)} %get-tuple-element.19), channel_id=1, source_target_pairs={{0,1},{1,0},{2,3},{3,2},{4,5},{5,4},{6,7},{7,6},{8,9},{9,8},{10,11... | collective-permute-start | bytes 196616 | tf_op jit(solution)/shard_map/ppermute | solution.py:204
  5.9 7.3 %collective-permute-start.1 = (bf16[4,64,128]{2,1,0:T(8,128)(2,1)S(1)}, bf16[4,64,128]{2,1,0:T(8,128)(2,1)S(1)}, u32[]{:S(2)}, u32[]{:S(2)}) collective-permute-start(bf16[4,64,128]{2,1,0:T(8,128)(2,1)S(1)} %get-tuple-element.20), channel_id=1, source_target_pairs={{0,2},{1,3},{2,0},{3,1},{4,6},{5,7},{6,4},{7,5},{8,10},{9,11},{10,... | collective-permute-start | bytes 196616 | tf_op jit(solution)/shard_map/ppermute | solution.py:204
  8.4 6.1 %collective-permute-start.2 = (bf16[4,64,128]{2,1,0:T(8,128)(2,1)S(1)}, bf16[4,64,128]{2,1,0:T(8,128)(2,1)S(1)}, u32[]{:S(2)}, u32[]{:S(2)}) collective-permute-start(bf16[4,64,128]{2,1,0:T(8,128)(2,1)S(1)} %get-tuple-element.21), channel_id=1, source_target_pairs={{0,3},{1,2},{2,1},{3,0},{4,7},{5,6},{6,5},{7,4},{8,11},{9,10},{10,... | collective-permute-start | bytes 196616 | tf_op jit(solution)/shard_map/ppermute | solution.py:204
  14.6 10.5 %collective-permute-start.4 = (bf16[4,4,64,128]{3,2,1,0:T(8,128)(2,1)S(1)}, bf16[4,4,64,128]{3,2,1,0:T(8,128)(2,1)S(1)}, u32[]{:S(2)}, u32[]{:S(2)}) collective-permute-start(bf16[4,4,64,128]{3,2,1,0:T(8,128)(2,1)S(1)} %pad_maximum_fusion.1), channel_id=1, source_target_pairs={{4,8},{8,4},{12,16},{16,12},{20,24},{24,20},{5,9},{9,5},{13,17},{1... | collective-permute-start | bytes 786440 | tf_op jit(solution)/shard_map/ppermute | solution.py:211
  16.5 8.6 %collective-permute-start.3 = (bf16[4,4,64,128]{3,2,1,0:T(8,128)(2,1)S(1)}, bf16[4,4,64,128]{3,2,1,0:T(8,128)(2,1)S(1)}, u32[]{:S(2)}, u32[]{:S(2)}) collective-permute-start(bf16[4,4,64,128]{3,2,1,0:T(8,128)(2,1)S(1)} %pad_maximum_fusion.1), channel_id=1, source_target_pairs={{0,4},{4,0},{8,12},{12,8},{16,20},{20,16},{24,28},{28,24},{1,5},{5... | collective-permute-start | bytes 786440 | tf_op jit(solution)/shard_map/ppermute | solution.py:211
  27.6 4.5 %collective-permute-start.5 = (bf16[4,64,128]{2,1,0:T(8,128)(2,1)S(1)}, bf16[4,64,128]{2,1,0:T(8,128)(2,1)S(1)}, u32[]{:S(2)}, u32[]{:S(2)}) collective-permute-start(bf16[4,64,128]{2,1,0:T(8,128)(2,1)S(1)} %get-tuple-element.28), channel_id=1, source_target_pairs={{0,1},{1,0},{2,3},{3,2},{4,5},{5,4},{6,7},{7,6},{8,9},{9,8},{10,11... | collective-permute-start | bytes 196616 | tf_op jit(solution)/shard_map/ppermute | solution.py:204
  27.7 5.8 %collective-permute-start.6 = (bf16[4,64,128]{2,1,0:T(8,128)(2,1)S(1)}, bf16[4,64,128]{2,1,0:T(8,128)(2,1)S(1)}, u32[]{:S(2)}, u32[]{:S(2)}) collective-permute-start(bf16[4,64,128]{2,1,0:T(8,128)(2,1)S(1)} %get-tuple-element.29), channel_id=1, source_target_pairs={{0,2},{1,3},{2,0},{3,1},{4,6},{5,7},{6,4},{7,5},{8,10},{9,11},{10,... | collective-permute-start | bytes 196616 | tf_op jit(solution)/shard_map/ppermute | solution.py:204
  30.0 6.1 %collective-permute-start.7 = (bf16[4,64,128]{2,1,0:T(8,128)(2,1)S(1)}, bf16[4,64,128]{2,1,0:T(8,128)(2,1)S(1)}, u32[]{:S(2)}, u32[]{:S(2)}) collective-permute-start(bf16[4,64,128]{2,1,0:T(8,128)(2,1)S(1)} %get-tuple-element.30), channel_id=1, source_target_pairs={{0,3},{1,2},{2,1},{3,0},{4,7},{5,6},{6,5},{7,4},{8,11},{9,10},{10,... | collective-permute-start | bytes 196616 | tf_op jit(solution)/shard_map/ppermute | solution.py:204

commit v3 on v2

--- a/solution.py
+++ b/solution.py
@@ -54,15 +54,6 @@
     return jnp.concatenate([block, turned(block)], 0)
 
 
-def lesser_of(blocks, chosen):
-    total = None
-    for block, other in zip(blocks, chosen):
-        half = jnp.dot(block, widened(other), preferred_element_type=F32).astype(BF16)
-        term = lax.dot_general(half, widened(block), NT, preferred_element_type=F32)
-        total = term if total is None else total + term
-    return total.astype(BF16)
-
-
 def opened():
     def kernel(out):
         out[...] = jnp.zeros_like(out)
@@ -80,29 +71,58 @@
 def lesser_blocks(n, per, opening, neighbours, green, sigma):
     _, _, terms, orb, wide = green.shape
 
-    def kernel(opening, neighbours, green, sigma, *outs):
+    def kernel(opening, neighbours, green, sigma, *rest):
+        outs, (table, halves, done) = rest[:n], rest[n:]
         me = lax.axis_index("eloc")
-        for k in range(n - 1, -1, -1):
-            for i in range(per):
-                atom = target_at(me, k, n) * per + i
-                chosen = [sigma[0, atom]] + [sigma[0, neighbours[j, atom]] for j in range(terms - 1)]
-                outs[k][i] = lesser_of([green[0, atom, j] for j in range(terms)], chosen)
+        copy = pltpu.make_async_copy(neighbours, table, done)
+        copy.start()
+        spots = [(k, i, target_at(me, k, n) * per + i) for k in range(n - 1, -1, -1) for i in range(per)]
+
+        def put_half(spot, j, other):
+            k, i, atom = spot
+            half = jnp.dot(green[0, atom, j], widened(sigma[0, other]), preferred_element_type=F32)
+            half = half.astype(BF16)
+            halves[k, i, j, :orb] = half
+            halves[k, i, j, orb:] = turned(half)
+
+        for spot in spots:
+            put_half(spot, 0, spot[2])
+        copy.wait()
+        for spot in spots:
+            for j in range(1, terms):
+                put_half(spot, j, table[j - 1, spot[2]])
+        for k, i, atom in spots:
+            total = None
+            for j in range(terms):
+                term = lax.dot_general(halves[k, i, j], green[0, atom, j], NT, preferred_element_type=F32)
+                total = term if total is None else total + term
+            outs[k][i] = jnp.concatenate([total[:orb], -total[orb:]], 1).astype(BF16)
 
     return pl.pallas_call(
         kernel,
         name="lesser",
         out_shape=[jax.ShapeDtypeStruct((per, orb, wide), BF16) for _ in range(n)],
-        in_specs=[VMEM, SMEM, VMEM, VMEM],
+        in_specs=[VMEM, HBM, VMEM, VMEM],
         out_specs=[VMEM for _ in range(n)],
+        scratch_shapes=[
+            pltpu.SMEM(neighbours.shape, jnp.int32),
+            pltpu.VMEM((n, per, terms, 2 * orb, wide), BF16),
+            pltpu.SemaphoreType.DMA,
+        ],
         compiler_params=limited(),
         cost_estimate=cost(400_000_000),
     )(opening, neighbours, green, sigma)
 
 
-def prepared(occupancy, couplings):
+def prepared(occupancy, shifts, couplings):
     modes, per, orb, wide = couplings.shape
 
-    def kernel(occupancy, couplings, right, left):
+    def kernel(occupancy, shifts, couplings, right, left, moves):
+        lane = lax.broadcasted_iota(jnp.int32, moves.shape, 1)
+        row = jnp.zeros(moves.shape, jnp.int32)
+        for m in range(modes):
+            row = jnp.where(lane == m, shifts[m], row)
+        moves[...] = row
         for a in range(per):
             for m in range(modes):
                 block = couplings[m, a]
@@ -119,23 +139,27 @@
         out_shape=[
             jax.ShapeDtypeStruct((per, modes, 2 * wide, wide), BF16),
             jax.ShapeDtypeStruct((per, 2 * orb, modes * orb), BF16),
+            jax.ShapeDtypeStruct((8, 128), jnp.int32),
         ],
-        in_specs=[SMEM, VMEM],
-        out_specs=[VMEM, VMEM],
+        in_specs=[SMEM, SMEM, VMEM],
+        out_specs=[VMEM, VMEM, VMEM],
         compiler_params=limited(),
         cost_estimate=cost(200_000_000),
-    )(occupancy, couplings)
-
-
-def mode_blocks(n, ks, shifts, extended, right, left):
+    )(occupancy, shifts, couplings)
+
+
+def mode_blocks(n, ks, moves, extended, right, left):
     per, modes, _, wide = right.shape
     orb = wide // 2
     width = 2 if len(ks) % 2 == 0 else 1
 
-    def kernel(shifts, extended, right, left, *rest):
+    def kernel(moves, extended, right, left, *rest):
         outs, stack = rest[: len(ks)], rest[-1]
         me = lax.axis_index("eloc")
         even = lax.axis_index("egrp") & 1 == 0
+        row = moves[...]
+        lane = lax.broadcasted_iota(jnp.int32, row.shape, 1)
+        shifts = [jnp.max(jnp.where(lane == m, row, 0)) for m in range(modes)]
         places = {}
         for m in range(modes):
             for k in ks:
@@ -166,12 +190,12 @@
     return pl.pallas_call(
         kernel,
         out_shape=[jax.ShapeDtypeStruct((per, orb, wide), BF16) for _ in ks],
-        in_specs=[SMEM, VMEM, VMEM, VMEM],
+        in_specs=[VMEM, VMEM, VMEM, VMEM],
         out_specs=[VMEM for _ in ks],
         scratch_shapes=[pltpu.VMEM((per, len(ks) // width, modes * orb, width * wide), BF16)],
         compiler_params=limited(),
         cost_estimate=cost(400_000_000),
-    )(shifts, extended, right, left)
+    )(moves, extended, right, left)
 
 
 def joined(n, blocks):
@@ -216,14 +240,16 @@
     per = couplings.shape[1]
     made = lesser_blocks(n, per, opened(), neighbours.T, green_blocks, sigma_prev)
     held = [made[0]] + [swapped(n, k, made[k]) for k in range(1, n)]
-    right, left = prepared(occupancy, couplings)
+    right, left, moves = prepared(occupancy, shifts, couplings)
+    soon = jnp.stack(held[: n // 2])
+    early = traded(groups, 1, soon)
     here = jnp.stack(held)
-    here, right, left = lax.optimization_barrier((here, right, left))
-    outer = traded(groups, 1, here)
+    here, right, left, moves = lax.optimization_barrier((here, right, left, moves))
+    outer = traded(groups, 1, here[n // 2 :])
     inner = traded(groups, 0, here)
-    extended = jnp.concatenate([inner, here, outer], 0)
+    extended = jnp.concatenate([inner, here, early, outer], 0)
     order = list(range(n - 1, -1, -1))
-    made = mode_blocks(n, order, shifts, extended, right, left)[::-1]
+    made = mode_blocks(n, order, moves, extended, right, left)[::-1]
     back = [made[0]] + [swapped(n, k, made[k]) for k in range(1, n)]
     return joined(n, back)
 

time: 37 us -> 36.4 us (0.984)
  starting transfers between devices: 12.5 us -> 15.4 us
  waiting for transfers between devices: 15.3 us -> 13.3 us
  Pallas kernels: 7.58 us -> 6.02 us
    ppermute x2 -> x3, starting transfers between devices: 3.58 us -> 6.53 us  [traded(): return lax.ppermute(block, 'egrp', pairs)]
    ppermute x2 -> x3, waiting for transfers between devices: 6.91 us -> 4.86 us  [traded(): return lax.ppermute(block, 'egrp', pairs)]
    pallas_call x1, Pallas kernels: 2.96 us -> 1.71 us  [lesser_blocks(): pl.pallas_call(kernel, name='lesser', out_shape=[jax.ShapeDtypeStruct((pe...]
  transfers between devices with their start and end apart: 8 -> 9, of which waited for: 5 -> 6; matrix products, arithmetic and copies ran while one was open for 0% -> 0% of each run, Pallas kernels for 4% -> 4%
where the time goes in v3:
time: 36.4 us; the launch traced here: 36.2 us
  starting transfers between devices  15.4 us (42%)
  waiting for transfers between devices  13.3 us (37%)
  Pallas kernels  6.02 us (17%)
  local copies, waits for them, and re-layouts  1.21 us (3%)
    ppermute x6, starting transfers between devices, swapped(): lax.ppermute(block, 'eloc', [(i, partner(i, k, n)) for i in range(n)])  8.9 us
    ppermute x6, waiting for transfers between devices, swapped(): lax.ppermute(block, 'eloc', [(i, partner(i, k, n)) for i in range(n)])  8.39 us
    ppermute x3, starting transfers between devices, traded(): return lax.ppermute(block, 'egrp', pairs)  6.53 us
    ppermute x3, waiting for transfers between devices, traded(): return lax.ppermute(block, 'egrp', pairs)  4.86 us
    pallas_call x1, Pallas kernels, mode_blocks(): pl.pallas_call(kernel, out_shape=[jax.ShapeDtypeStruct((per, orb, wide),...  2.13 us
    pallas_call x1, Pallas kernels, lesser_blocks(): pl.pallas_call(kernel, name='lesser', out_shape=[jax.ShapeDtypeStruct((pe...  1.71 us
    pallas_call x1, Pallas kernels, prepared(): pl.pallas_call(kernel, name='prepare', out_shape=[jax.ShapeDtypeStruct((p...  1.45 us
    unnamed x12, local copies, waits for them, and re-layouts  1.2 us
  transfers between devices with their start and end apart: 9, of which 6 were waited for; matrix products, arithmetic and copies ran while one was open for 0% of the time, Pallas kernels for 4%

profile of v3, /device:TPU:4, one launch (start us, length us, event | category | flops | bytes accessed | tf_op | source)
XLA Modules:
  0.0 36.2 jit_solution(528510552560183300)
XLA Ops:
  0.0 0.6 %copy-done.3 = s32[16,2]{0,1:T(2,128)S(1)} copy-done((s32[16,2]{0,1:T(2,128)S(1)}, s32[16,2]{0,1:T(2,128)}, u32[]{:S(2)}) %copy-start.3) | copy-done | bytes 152
  0.7 0.3 copy-done.2
  1.0 0.3 copy-done
  1.2 1.7 %lesser.1 = (bf16[4,64,128]{2,1,0:T(8,128)(2,1)S(1)}, bf16[4,64,128]{2,1,0:T(8,128)(2,1)S(1)}, bf16[4,64,128]{2,1,0:T(8,128)(2,1)S(1)}, bf16[4,64,128]{2,1,0:T(8,128)(2,1)S(1)}) custom-call(s32[8,128]{1,0:T(8,128)S(1)} %opening.1, s32[2,16]{1,0:T(2,128)S(1)} %bitcast.7, bf16[1,16,3,64,128]{4,3,2,1,0:T(8,128)(2,1)S(1)} %copy-done, ...), custom_call_target="tpu_custom_call" | custom-call | flops 400000000 | bytes 1000000 | tf_op jit(solution)/shard_map/lesser/pallas_call | solution.py:101
  2.9 1.6 %collective-permute-start = (bf16[4,64,128]{2,1,0:T(8,128)(2,1)S(1)}, bf16[4,64,128]{2,1,0:T(8,128)(2,1)S(1)}, u32[]{:S(2)}, u32[]{:S(2)}) collective-permute-start(bf16[4,64,128]{2,1,0:T(8,128)(2,1)S(1)} %get-tuple-element.21), channel_id=1, source_target_pairs={{0,1},{1,0},{2,3},{3,2},{4,5},{5,4},{6,7},{7,6},{8,9},{9,8},{10,11... | collective-permute-start | bytes 196616 | tf_op jit(solution)/shard_map/ppermute | solution.py:228
  4.6 2.6 %collective-permute-start.1 = (bf16[4,64,128]{2,1,0:T(8,128)(2,1)S(1)}, bf16[4,64,128]{2,1,0:T(8,128)(2,1)S(1)}, u32[]{:S(2)}, u32[]{:S(2)}) collective-permute-start(bf16[4,64,128]{2,1,0:T(8,128)(2,1)S(1)} %get-tuple-element.22), channel_id=1, source_target_pairs={{0,2},{1,3},{2,0},{3,1},{4,6},{5,7},{6,4},{7,5},{8,10},{9,11},{10,... | collective-permute-start | bytes 196616 | tf_op jit(solution)/shard_map/ppermute | solution.py:228
  7.2 0.2 collective-permute-start.2
  7.4 1.5 %prepare.1 = (bf16[4,6,256,128]{3,2,1,0:T(8,128)(2,1)S(1)}, bf16[4,128,384]{2,1,0:T(8,128)(2,1)S(1)}, s32[8,128]{1,0:T(8,128)S(1)}) custom-call(f32[6]{0:T(128)S(1)} %copy-done.4, s32[6]{0:T(128)S(1)} %copy-done.5, bf16[6,4,64,128]{3,2,1,0:T(8,128)(2,1)S(1)} %copy-done.1), custom_call_target="tpu_custom_call" | custom-call | flops 200000000 | bytes 1000000 | tf_op jit(solution)/shard_map/prepare/pallas_call | solution.py:136
  8.9 0.0 collective-permute-done
  8.9 3.0 %collective-permute-done.1 = bf16[4,64,128]{2,1,0:T(8,128)(2,1)S(1)} collective-permute-done((bf16[4,64,128]{2,1,0:T(8,128)(2,1)S(1)}, bf16[4,64,128]{2,1,0:T(8,128)(2,1)S(1)}, u32[]{:S(2)}, u32[]{:S(2)}) %collective-permute-start.1) | collective-permute-done | bytes 65568 | tf_op jit(solution)/shard_map/ppermute | solution.py:228
  11.8 1.4 %collective-permute-done.2 = bf16[4,64,128]{2,1,0:T(8,128)(2,1)S(1)} collective-permute-done((bf16[4,64,128]{2,1,0:T(8,128)(2,1)S(1)}, bf16[4,64,128]{2,1,0:T(8,128)(2,1)S(1)}, u32[]{:S(2)}, u32[]{:S(2)}) %collective-permute-start.2) | collective-permute-done | bytes 65568 | tf_op jit(solution)/shard_map/ppermute | solution.py:228
  13.3 0.1 collective-permute-start.3
  13.4 3.4 %collective-permute-start.4 = (bf16[2,4,64,128]{3,2,1,0:T(8,128)(2,1)S(1)}, bf16[2,4,64,128]{3,2,1,0:T(8,128)(2,1)S(1)}, u32[]{:S(2)}, u32[]{:S(2)}) collective-permute-start(bf16[2,4,64,128]{3,2,1,0:T(8,128)(2,1)S(1)} %pad_maximum_fusion.2), channel_id=1, source_target_pairs={{4,8},{8,4},{12,16},{16,12},{20,24},{24,20},{5,9},{9,5},{13,17},{1... | collective-permute-start | bytes 393224 | tf_op jit(solution)/shard_map/ppermute | solution.py:235
  16.9 3.0 %collective-permute-start.5 = (bf16[2,4,64,128]{3,2,1,0:T(8,128)(2,1)S(1)}, bf16[2,4,64,128]{3,2,1,0:T(8,128)(2,1)S(1)}, u32[]{:S(2)}, u32[]{:S(2)}) collective-permute-start(bf16[2,4,64,128]{3,2,1,0:T(8,128)(2,1)S(1)} %slice.3), channel_id=1, source_target_pairs={{4,8},{8,4},{12,16},{16,12},{20,24},{24,20},{5,9},{9,5},{13,17},{1... | collective-permute-start | bytes 393224 | tf_op jit(solution)/shard_map/ppermute | solution.py:235
  19.9 1.8 %collective-permute-done.4 = bf16[2,4,64,128]{3,2,1,0:T(8,128)(2,1)S(1)} collective-permute-done((bf16[2,4,64,128]{3,2,1,0:T(8,128)(2,1)S(1)}, bf16[2,4,64,128]{3,2,1,0:T(8,128)(2,1)S(1)}, u32[]{:S(2)}, u32[]{:S(2)}) %collective-permute-start.4) | collective-permute-done | bytes 131104 | tf_op jit(solution)/shard_map/ppermute | solution.py:235
  21.7 3.0 %collective-permute-done.5 = bf16[2,4,64,128]{3,2,1,0:T(8,128)(2,1)S(1)} collective-permute-done((bf16[2,4,64,128]{3,2,1,0:T(8,128)(2,1)S(1)}, bf16[2,4,64,128]{3,2,1,0:T(8,128)(2,1)S(1)}, u32[]{:S(2)}, u32[]{:S(2)}) %collective-permute-start.5) | collective-permute-done | bytes 131104 | tf_op jit(solution)/shard_map/ppermute | solution.py:235
  24.8 0.1 pad_maximum_fusion.extended
  24.9 2.1 %shard_map.64 = (bf16[4,64,128]{2,1,0:T(8,128)(2,1)S(1)}, bf16[4,64,128]{2,1,0:T(8,128)(2,1)S(1)}, bf16[4,64,128]{2,1,0:T(8,128)(2,1)S(1)}, bf16[4,64,128]{2,1,0:T(8,128)(2,1)S(1)}) custom-call(s32[8,128]{1,0:T(8,128)S(1)} %get-tuple-element.27.moves, bf16[12,4,64,128]{3,2,1,0:T(8,128)(2,1)S(1)} %pad_maximum_fusion.extended, ...), custom_call_target="tpu_custom_call" | custom-call | flops 400000000 | bytes 1000000 | tf_op jit(solution)/shard_map/pallas_call | solution.py:190
  27.0 0.1 collective-permute-start.6
  27.1 2.3 %collective-permute-start.7 = (bf16[4,64,128]{2,1,0:T(8,128)(2,1)S(1)}, bf16[4,64,128]{2,1,0:T(8,128)(2,1)S(1)}, u32[]{:S(2)}, u32[]{:S(2)}) collective-permute-start(bf16[4,64,128]{2,1,0:T(8,128)(2,1)S(1)} %get-tuple-element.33), channel_id=1, source_target_pairs={{0,2},{1,3},{2,0},{3,1},{4,6},{5,7},{6,4},{7,5},{8,10},{9,11},{10,... | collective-permute-start | bytes 196616 | tf_op jit(solution)/shard_map/ppermute | solution.py:228
  29.4 2.0 %collective-permute-start.8 = (bf16[4,64,128]{2,1,0:T(8,128)(2,1)S(1)}, bf16[4,64,128]{2,1,0:T(8,128)(2,1)S(1)}, u32[]{:S(2)}, u32[]{:S(2)}) collective-permute-start(bf16[4,64,128]{2,1,0:T(8,128)(2,1)S(1)} %get-tuple-element.34), channel_id=1, source_target_pairs={{0,3},{1,2},{2,1},{3,0},{4,7},{5,6},{6,5},{7,4},{8,11},{9,10},{10,... | collective-permute-start | bytes 196616 | tf_op jit(solution)/shard_map/ppermute | solution.py:228
  31.5 2.6 %collective-permute-done.7.refs_2_ = bf16[4,64,128]{2,1,0:T(8,128)(2,1)S(1)} collective-permute-done((bf16[4,64,128]{2,1,0:T(8,128)(2,1)S(1)}, bf16[4,64,128]{2,1,0:T(8,128)(2,1)S(1)}, u32[]{:S(2)}, u32[]{:S(2)}) %collective-permute-start.7) | collective-permute-done | bytes 65568 | tf_op jit(solution)/shard_map/ppermute | solution.py:228
  34.0 1.5 %collective-permute-done.8.refs_3_ = bf16[4,64,128]{2,1,0:T(8,128)(2,1)S(1)} collective-permute-done((bf16[4,64,128]{2,1,0:T(8,128)(2,1)S(1)}, bf16[4,64,128]{2,1,0:T(8,128)(2,1)S(1)}, u32[]{:S(2)}, u32[]{:S(2)}) %collective-permute-start.8) | collective-permute-done | bytes 65568 | tf_op jit(solution)/shard_map/ppermute | solution.py:228
  35.5 0.7 %join.1 = bf16[1,16,64,128]{3,2,1,0:T(8,128)(2,1)} custom-call(bf16[4,64,128]{2,1,0:T(8,128)(2,1)S(1)} %get-tuple-element.31.refs_0_, bf16[4,64,128]{2,1,0:T(8,128)(2,1)S(1)} %collective-permute-done.6.refs_1_, bf16[4,64,128]{2,1,0:T(8,128)(2,1)S(1)} %collective-permute-done.7.refs_2_, bf16[4,64,128]{2,1,0:T(8,128)(2,1)S(1)} %collective-permute-done.8.refs_3_), custom_call_target="tpu_custom_call" | custom-call | tf_op jit(solution)/shard_map/join/pallas_call | solution.py:216
  (15 shorter events, 0.1 us)
Async XLA Ops:
  0.0 0.7 %copy-start.3 = (s32[16,2]{0,1:T(2,128)S(1)}, s32[16,2]{0,1:T(2,128)}, u32[]{:S(2)}) copy-start(s32[16,2]{0,1:T(2,128)} %param.8) | copy-start | bytes 388
  0.0 1.0 %copy-start.2 = (bf16[1,16,64,128]{3,2,1,0:T(8,128)(2,1)S(1)}, bf16[1,16,64,128]{3,2,1,0:T(8,128)(2,1)}, u32[]{:S(2)}) copy-start(bf16[1,16,64,128]{3,2,1,0:T(8,128)(2,1)} %sigma.1) | copy-start | bytes 786436
  0.0 1.2 %copy-start = (bf16[1,16,3,64,128]{4,3,2,1,0:T(8,128)(2,1)S(1)}, bf16[1,16,3,64,128]{4,3,2,1,0:T(8,128)(2,1)}, u32[]{:S(2)}) copy-start(bf16[1,16,3,64,128]{4,3,2,1,0:T(8,128)(2,1)} %green.1) | copy-start | bytes 2359300
  0.0 7.4 %copy-start.5 = (s32[6]{0:T(128)S(1)}, s32[6]{0:T(128)}, u32[]{:S(2)}) copy-start(s32[6]{0:T(128)} %shifts.1) | copy-start | bytes 76
  0.0 7.4 %copy-start.4 = (f32[6]{0:T(128)S(1)}, f32[6]{0:T(128)}, u32[]{:S(2)}) copy-start(f32[6]{0:T(128)} %occupancy.1) | copy-start | bytes 76
  0.0 7.4 %copy-start.1 = (bf16[6,4,64,128]{3,2,1,0:T(8,128)(2,1)S(1)}, bf16[6,4,64,128]{3,2,1,0:T(8,128)(2,1)}, u32[]{:S(2)}) copy-start(bf16[6,4,64,128]{3,2,1,0:T(8,128)(2,1)} %couplings.1) | copy-start | bytes 1179652
  2.9 5.9 %collective-permute-start = (bf16[4,64,128]{2,1,0:T(8,128)(2,1)S(1)}, bf16[4,64,128]{2,1,0:T(8,128)(2,1)S(1)}, u32[]{:S(2)}, u32[]{:S(2)}) collective-permute-start(bf16[4,64,128]{2,1,0:T(8,128)(2,1)S(1)} %get-tuple-element.21), channel_id=1, source_target_pairs={{0,1},{1,0},{2,3},{3,2},{4,5},{5,4},{6,7},{7,6},{8,9},{9,8},{10,11... | collective-permute-start | bytes 196616 | tf_op jit(solution)/shard_map/ppermute | solution.py:228
  4.6 7.3 %collective-permute-start.1 = (bf16[4,64,128]{2,1,0:T(8,128)(2,1)S(1)}, bf16[4,64,128]{2,1,0:T(8,128)(2,1)S(1)}, u32[]{:S(2)}, u32[]{:S(2)}) collective-permute-start(bf16[4,64,128]{2,1,0:T(8,128)(2,1)S(1)} %get-tuple-element.22), channel_id=1, source_target_pairs={{0,2},{1,3},{2,0},{3,1},{4,6},{5,7},{6,4},{7,5},{8,10},{9,11},{10,... | collective-permute-start | bytes 196616 | tf_op jit(solution)/shard_map/ppermute | solution.py:228
  7.2 6.1 %collective-permute-start.2 = (bf16[4,64,128]{2,1,0:T(8,128)(2,1)S(1)}, bf16[4,64,128]{2,1,0:T(8,128)(2,1)S(1)}, u32[]{:S(2)}, u32[]{:S(2)}) collective-permute-start(bf16[4,64,128]{2,1,0:T(8,128)(2,1)S(1)} %get-tuple-element.23), channel_id=1, source_target_pairs={{0,3},{1,2},{2,1},{3,0},{4,7},{5,6},{6,5},{7,4},{8,11},{9,10},{10,... | collective-permute-start | bytes 196616 | tf_op jit(solution)/shard_map/ppermute | solution.py:228
  13.3 11.5 %collective-permute-start.3 = (bf16[4,4,64,128]{3,2,1,0:T(8,128)(2,1)S(1)}, bf16[4,4,64,128]{3,2,1,0:T(8,128)(2,1)S(1)}, u32[]{:S(2)}, u32[]{:S(2)}) collective-permute-start(bf16[4,4,64,128]{3,2,1,0:T(8,128)(2,1)S(1)} %pad_maximum_fusion.1), channel_id=1, source_target_pairs={{0,4},{4,0},{8,12},{12,8},{16,20},{20,16},{24,28},{28,24},{1,5},{5... | collective-permute-start | bytes 786440 | tf_op jit(solution)/shard_map/ppermute | solution.py:235
  13.4 8.3 %collective-permute-start.4 = (bf16[2,4,64,128]{3,2,1,0:T(8,128)(2,1)S(1)}, bf16[2,4,64,128]{3,2,1,0:T(8,128)(2,1)S(1)}, u32[]{:S(2)}, u32[]{:S(2)}) collective-permute-start(bf16[2,4,64,128]{3,2,1,0:T(8,128)(2,1)S(1)} %pad_maximum_fusion.2), channel_id=1, source_target_pairs={{4,8},{8,4},{12,16},{16,12},{20,24},{24,20},{5,9},{9,5},{13,17},{1... | collective-permute-start | bytes 393224 | tf_op jit(solution)/shard_map/ppermute | solution.py:235
  16.9 7.9 %collective-permute-start.5 = (bf16[2,4,64,128]{3,2,1,0:T(8,128)(2,1)S(1)}, bf16[2,4,64,128]{3,2,1,0:T(8,128)(2,1)S(1)}, u32[]{:S(2)}, u32[]{:S(2)}) collective-permute-start(bf16[2,4,64,128]{3,2,1,0:T(8,128)(2,1)S(1)} %slice.3), channel_id=1, source_target_pairs={{4,8},{8,4},{12,16},{16,12},{20,24},{24,20},{5,9},{9,5},{13,17},{1... | collective-permute-start | bytes 393224 | tf_op jit(solution)/shard_map/ppermute | solution.py:235
  27.0 4.5 %collective-permute-start.6 = (bf16[4,64,128]{2,1,0:T(8,128)(2,1)S(1)}, bf16[4,64,128]{2,1,0:T(8,128)(2,1)S(1)}, u32[]{:S(2)}, u32[]{:S(2)}) collective-permute-start(bf16[4,64,128]{2,1,0:T(8,128)(2,1)S(1)} %get-tuple-element.32), channel_id=1, source_target_pairs={{0,1},{1,0},{2,3},{3,2},{4,5},{5,4},{6,7},{7,6},{8,9},{9,8},{10,11... | collective-permute-start | bytes 196616 | tf_op jit(solution)/shard_map/ppermute | solution.py:228
  27.1 6.9 %collective-permute-start.7 = (bf16[4,64,128]{2,1,0:T(8,128)(2,1)S(1)}, bf16[4,64,128]{2,1,0:T(8,128)(2,1)S(1)}, u32[]{:S(2)}, u32[]{:S(2)}) collective-permute-start(bf16[4,64,128]{2,1,0:T(8,128)(2,1)S(1)} %get-tuple-element.33), channel_id=1, source_target_pairs={{0,2},{1,3},{2,0},{3,1},{4,6},{5,7},{6,4},{7,5},{8,10},{9,11},{10,... | collective-permute-start | bytes 196616 | tf_op jit(solution)/shard_map/ppermute | solution.py:228
  29.4 6.1 %collective-permute-start.8 = (bf16[4,64,128]{2,1,0:T(8,128)(2,1)S(1)}, bf16[4,64,128]{2,1,0:T(8,128)(2,1)S(1)}, u32[]{:S(2)}, u32[]{:S(2)}) collective-permute-start(bf16[4,64,128]{2,1,0:T(8,128)(2,1)S(1)} %get-tuple-element.34), channel_id=1, source_target_pairs={{0,3},{1,2},{2,1},{3,0},{4,7},{5,6},{6,5},{7,4},{8,11},{9,10},{10,... | collective-permute-start | bytes 196616 | tf_op jit(solution)/shard_map/ppermute | solution.py:228

commit v4 on v3

--- a/solution.py
+++ b/solution.py
@@ -148,21 +148,43 @@
     )(occupancy, shifts, couplings)
 
 
-def mode_blocks(n, ks, moves, extended, right, left):
+def read_moves(moves, modes):
+    row = moves[...]
+    lane = lax.broadcasted_iota(jnp.int32, row.shape, 1)
+    return [jnp.max(jnp.where(lane == m, row, 0)) for m in range(modes)]
+
+
+def put_products(stack, a, m, product, count, width):
+    orb, wide = product.shape[0] // count, product.shape[1]
+    for q in range(count):
+        p, w = divmod(q, width)
+        stack[a, p, m * orb : (m + 1) * orb, w * wide : (w + 1) * wide] = product[q * orb : (q + 1) * orb]
+
+
+def outer_products(stack, left, a, count, width):
+    orb = left.shape[1] // 2
+    pieces = []
+    for p in range(count // width):
+        both = jnp.dot(left[a], stack[a, p], preferred_element_type=F32)
+        for w in range(width):
+            piece = both[:, w * 2 * orb : (w + 1) * 2 * orb]
+            pieces.append(piece[:orb] + turned(piece[orb:]))
+    return pieces
+
+
+def first_modes(n, moves, extended, right, left):
     per, modes, _, wide = right.shape
     orb = wide // 2
-    width = 2 if len(ks) % 2 == 0 else 1
+    width = 2 if n % 2 == 0 else 1
 
     def kernel(moves, extended, right, left, *rest):
-        outs, stack = rest[: len(ks)], rest[-1]
+        outs, stack = rest[:n], rest[-1]
         me = lax.axis_index("eloc")
         even = lax.axis_index("egrp") & 1 == 0
-        row = moves[...]
-        lane = lax.broadcasted_iota(jnp.int32, row.shape, 1)
-        shifts = [jnp.max(jnp.where(lane == m, row, 0)) for m in range(modes)]
+        shifts = read_moves(moves, modes)
         places = {}
         for m in range(modes):
-            for k in ks:
+            for k in range(n):
                 e = target_at(me, k, n) + n
                 above, below = place_of(me, e + shifts[m], n), place_of(me, e - shifts[m], n)
                 above = jnp.where(even & (above >= 2 * n), above - 2 * n, above)
@@ -170,32 +192,71 @@
                 places[m, k] = (above, below)
         for a in range(per):
             for m in range(modes):
+                rows = [
+                    jnp.concatenate([extended[places[m, k][0], a], extended[places[m, k][1], a]], 1)
+                    for k in range(n)
+                ]
+                product = jnp.dot(jnp.concatenate(rows, 0), right[a, m], preferred_element_type=F32)
+                put_products(stack, a, m, product.astype(BF16), n, width)
+            for k, piece in enumerate(outer_products(stack, left, a, n, width)):
+                outs[k][a] = piece
+
+    return pl.pallas_call(
+        kernel,
+        name="first_modes",
+        out_shape=[jax.ShapeDtypeStruct((per, orb, wide), F32) for _ in range(n)],
+        in_specs=[VMEM for _ in range(4)],
+        out_specs=[VMEM for _ in range(n)],
+        scratch_shapes=[pltpu.VMEM((per, n // width, modes * orb, width * wide), BF16)],
+        compiler_params=limited(),
+        cost_estimate=cost(400_000_000),
+    )(moves, extended, right, left)
+
+
+def last_modes(n, groups, ks, moves, outer, partials, right, left):
+    per, modes, _, wide = right.shape
+    orb, count, late = wide // 2, len(ks), n - outer.shape[0]
+    width = 2 if count % 2 == 0 else 1
+
+    def kernel(moves, outer, right, left, *rest):
+        partials, outs, stack = rest[:count], rest[count : 2 * count], rest[-1]
+        me = lax.axis_index("eloc")
+        even = lax.axis_index("egrp") & 1 == 0
+        group = lax.axis_index("egrp")
+        within = (group > 0) & (group < groups - 1)
+        begin = pl.multiple_of(jnp.where(even, wide, 0), wide)
+        shifts = read_moves(moves, modes)
+        places = {}
+        for m in range(modes):
+            for k in ks:
+                e = target_at(me, k, n) + n
+                t = jnp.where(even, e - shifts[m], e + shifts[m])
+                outside = jnp.where(even, t < n, t >= 2 * n) & within
+                base = jnp.where(even, 0, 2 * n)
+                slot = jnp.where(outside, place_of(me, t, n) - base, 0)
+                places[m, k] = (slot >= late, jnp.maximum(slot - late, 0))
+        for a in range(per):
+            for m in range(modes):
                 rows = []
                 for k in ks:
-                    above, below = places[m, k]
-                    rows.append(jnp.concatenate([extended[above, a], extended[below, a]], 1))
-                stacked = jnp.concatenate(rows, 0)
-                product = jnp.dot(stacked, right[a, m], preferred_element_type=F32).astype(BF16)
-                for q in range(len(ks)):
-                    p, w = divmod(q, width)
-                    stack[a, p, m * orb : (m + 1) * orb, w * wide : (w + 1) * wide] = (
-                        product[q * orb : (q + 1) * orb]
-                    )
-            for p in range(len(ks) // width):
-                both = jnp.dot(left[a], stack[a, p], preferred_element_type=F32)
-                for w in range(width):
-                    piece = both[:, w * wide : (w + 1) * wide]
-                    outs[p * width + w][a] = (piece[:orb] + turned(piece[orb:])).astype(BF16)
+                    held, slot = places[m, k]
+                    block = outer[slot, a]
+                    rows.append(jnp.where(held, block, jnp.zeros_like(block)))
+                weights = right[a, m, pl.ds(begin, wide)]
+                product = jnp.dot(jnp.concatenate(rows, 0), weights, preferred_element_type=F32)
+                put_products(stack, a, m, product.astype(BF16), count, width)
+            for q, piece in enumerate(outer_products(stack, left, a, count, width)):
+                outs[q][a] = (partials[q][a] + piece).astype(BF16)
 
     return pl.pallas_call(
         kernel,
         out_shape=[jax.ShapeDtypeStruct((per, orb, wide), BF16) for _ in ks],
-        in_specs=[VMEM, VMEM, VMEM, VMEM],
+        in_specs=[VMEM for _ in range(4 + count)],
         out_specs=[VMEM for _ in ks],
-        scratch_shapes=[pltpu.VMEM((per, len(ks) // width, modes * orb, width * wide), BF16)],
+        scratch_shapes=[pltpu.VMEM((per, count // width, modes * orb, width * wide), BF16)],
         compiler_params=limited(),
         cost_estimate=cost(400_000_000),
-    )(moves, extended, right, left)
+    )(moves, outer, right, left, *[partials[k] for k in ks])
 
 
 def joined(n, blocks):
@@ -230,9 +291,15 @@
 
 def traded(groups, first, block):
     pairs = []
-    for i in range(first, groups - 1, 2):
-        pairs += [(i, i + 1), (i + 1, i)]
+    for i in range(first, groups - 1 + (groups % 2 == 0) * first, 2):
+        pairs += [(i, (i + 1) % groups), ((i + 1) % groups, i)]
     return lax.ppermute(block, "egrp", pairs)
+
+
+def inside(groups, block):
+    me = lax.axis_index("egrp")
+    edge = (me == 0) | (me == groups - 1)
+    return jnp.where(edge, jnp.zeros_like(block), block)
 
 
 def shards(green_blocks, sigma_prev, neighbours, couplings, occupancy, shifts):
@@ -247,10 +314,14 @@
     here, right, left, moves = lax.optimization_barrier((here, right, left, moves))
     outer = traded(groups, 1, here[n // 2 :])
     inner = traded(groups, 0, here)
-    extended = jnp.concatenate([inner, here, early, outer], 0)
-    order = list(range(n - 1, -1, -1))
-    made = mode_blocks(n, order, moves, extended, right, left)[::-1]
-    back = [made[0]] + [swapped(n, k, made[k]) for k in range(1, n)]
+    missing = jnp.zeros_like(outer)
+    partials = first_modes(n, moves, jnp.concatenate([inner, here, inside(groups, early), missing], 0), right, left)
+    back = {}
+    for ks in (list(range(n)),):
+        made = last_modes(n, groups, ks, moves, outer, partials, right, left)
+        for k, block in zip(ks, made):
+            back[k] = swapped(n, k, block) if k else block
+    back = [back[k] for k in range(n)]
     return joined(n, back)
 
 

time: 36.4 us -> 32.3 us (0.89)
  the two profiles are of different devices: /device:TPU:4 before, /device:TPU:0 now
where the time goes in v4:
time: 32.3 us; the launch traced here: 32.2 us
  starting transfers between devices  14.2 us (44%)
  waiting for transfers between devices  8.68 us (27%)
  Pallas kernels  7.71 us (24%)
  local copies, waits for them, and re-layouts  1.21 us (4%)
    ppermute x6, starting transfers between devices, swapped(): lax.ppermute(block, 'eloc', [(i, partner(i, k, n)) for i in range(n)])  10.2 us
    ppermute x6, waiting for transfers between devices, swapped(): lax.ppermute(block, 'eloc', [(i, partner(i, k, n)) for i in range(n)])  7.55 us
    ppermute x3, starting transfers between devices, traded(): return lax.ppermute(block, 'egrp', pairs)  4.06 us
    pallas_call x1, Pallas kernels, first_modes(): pl.pallas_call(kernel, name='first_modes', out_shape=[jax.ShapeDtypeStruc...  2.13 us
    pallas_call x1, Pallas kernels, lesser_blocks(): pl.pallas_call(kernel, name='lesser', out_shape=[jax.ShapeDtypeStruct((pe...  1.71 us
    pallas_call x1, Pallas kernels, last_modes(): pl.pallas_call(kernel, out_shape=[jax.ShapeDtypeStruct((per, orb, wide),...  1.69 us
    pallas_call x1, Pallas kernels, prepared(): pl.pallas_call(kernel, name='prepare', out_shape=[jax.ShapeDtypeStruct((p...  1.45 us
    unnamed x12, local copies, waits for them, and re-layouts  1.18 us
  transfers between devices with their start and end apart: 9, of which 6 were waited for; matrix products, arithmetic and copies ran while one was open for 1% of the time, Pallas kernels for 11%

profile of v4, /device:TPU:0, one launch (start us, length us, event | category | flops | bytes accessed | tf_op | source)
XLA Modules:
  0.0 32.2 jit_solution(17441673417292708250)
XLA Ops:
  0.0 0.6 %copy-done.3 = s32[16,2]{0,1:T(2,128)S(1)} copy-done((s32[16,2]{0,1:T(2,128)S(1)}, s32[16,2]{0,1:T(2,128)}, u32[]{:S(2)}) %copy-start.3) | copy-done | bytes 152
  0.7 0.5 %copy-done = bf16[1,16,3,64,128]{4,3,2,1,0:T(8,128)(2,1)S(1)} copy-done((bf16[1,16,3,64,128]{4,3,2,1,0:T(8,128)(2,1)S(1)}, bf16[1,16,3,64,128]{4,3,2,1,0:T(8,128)(2,1)}, u32[]{:S(2)}) %copy-start) | copy-done | bytes 786456
  1.1 0.1 copy-done.2
  1.2 1.7 %lesser.1 = (bf16[4,64,128]{2,1,0:T(8,128)(2,1)S(1)}, bf16[4,64,128]{2,1,0:T(8,128)(2,1)S(1)}, bf16[4,64,128]{2,1,0:T(8,128)(2,1)S(1)}, bf16[4,64,128]{2,1,0:T(8,128)(2,1)S(1)}) custom-call(s32[8,128]{1,0:T(8,128)S(1)} %opening.1, s32[2,16]{1,0:T(2,128)S(1)} %bitcast.7, bf16[1,16,3,64,128]{4,3,2,1,0:T(8,128)(2,1)S(1)} %copy-done, ...), custom_call_target="tpu_custom_call" | custom-call | flops 400000000 | bytes 1000000 | tf_op jit(solution)/shard_map/lesser/pallas_call | solution.py:101
  2.9 3.1 %collective-permute-start = (bf16[4,64,128]{2,1,0:T(8,128)(2,1)S(1)}, bf16[4,64,128]{2,1,0:T(8,128)(2,1)S(1)}, u32[]{:S(2)}, u32[]{:S(2)}) collective-permute-start(bf16[4,64,128]{2,1,0:T(8,128)(2,1)S(1)} %get-tuple-element.25), channel_id=1, source_target_pairs={{0,1},{1,0},{2,3},{3,2},{4,5},{5,4},{6,7},{7,6},{8,9},{9,8},{10,11... | collective-permute-start | bytes 196616 | tf_op jit(solution)/shard_map/ppermute | solution.py:289
  6.0 2.6 %collective-permute-start.1 = (bf16[4,64,128]{2,1,0:T(8,128)(2,1)S(1)}, bf16[4,64,128]{2,1,0:T(8,128)(2,1)S(1)}, u32[]{:S(2)}, u32[]{:S(2)}) collective-permute-start(bf16[4,64,128]{2,1,0:T(8,128)(2,1)S(1)} %get-tuple-element.26), channel_id=1, source_target_pairs={{0,2},{1,3},{2,0},{3,1},{4,6},{5,7},{6,4},{7,5},{8,10},{9,11},{10,... | collective-permute-start | bytes 196616 | tf_op jit(solution)/shard_map/ppermute | solution.py:289
  8.6 0.0 collective-permute-start.2
  8.6 1.5 %prepare.1 = (bf16[4,6,256,128]{3,2,1,0:T(8,128)(2,1)S(1)}, bf16[4,128,384]{2,1,0:T(8,128)(2,1)S(1)}, s32[8,128]{1,0:T(8,128)S(1)}) custom-call(f32[6]{0:T(128)S(1)} %copy-done.4, s32[6]{0:T(128)S(1)} %copy-done.5, bf16[6,4,64,128]{3,2,1,0:T(8,128)(2,1)S(1)} %copy-done.1), custom_call_target="tpu_custom_call" | custom-call | flops 200000000 | bytes 1000000 | tf_op jit(solution)/shard_map/prepare/pallas_call | solution.py:136
  10.1 1.4 %collective-permute-start.5 = (bf16[2,4,64,128]{3,2,1,0:T(8,128)(2,1)S(1)}, bf16[2,4,64,128]{3,2,1,0:T(8,128)(2,1)S(1)}, u32[]{:S(2)}, u32[]{:S(2)}) collective-permute-start(bf16[2,4,64,128]{3,2,1,0:T(8,128)(2,1)S(1)} %pad_maximum_fusion.2), channel_id=1, source_target_pairs={{4,8},{8,4},{12,16},{16,12},{20,24},{24,20},{28,0},{0,28},{5,9},{9... | collective-permute-start | bytes 393224 | tf_op jit(solution)/shard_map/ppermute | solution.py:296
  11.5 1.8 %collective-permute-done.1 = bf16[4,64,128]{2,1,0:T(8,128)(2,1)S(1)} collective-permute-done((bf16[4,64,128]{2,1,0:T(8,128)(2,1)S(1)}, bf16[4,64,128]{2,1,0:T(8,128)(2,1)S(1)}, u32[]{:S(2)}, u32[]{:S(2)}) %collective-permute-start.1) | collective-permute-done | bytes 65568 | tf_op jit(solution)/shard_map/ppermute | solution.py:289
  13.3 1.4 %collective-permute-done.2 = bf16[4,64,128]{2,1,0:T(8,128)(2,1)S(1)} collective-permute-done((bf16[4,64,128]{2,1,0:T(8,128)(2,1)S(1)}, bf16[4,64,128]{2,1,0:T(8,128)(2,1)S(1)}, u32[]{:S(2)}, u32[]{:S(2)}) %collective-permute-start.2) | collective-permute-done | bytes 65568 | tf_op jit(solution)/shard_map/ppermute | solution.py:289
  14.7 0.1 collective-permute-start.4
  14.8 2.6 %collective-permute-start.3 = (bf16[2,4,64,128]{3,2,1,0:T(8,128)(2,1)S(1)}, bf16[2,4,64,128]{3,2,1,0:T(8,128)(2,1)S(1)}, u32[]{:S(2)}, u32[]{:S(2)}) collective-permute-start(bf16[2,4,64,128]{3,2,1,0:T(8,128)(2,1)S(1)} %slice.3), channel_id=1, source_target_pairs={{4,8},{8,4},{12,16},{16,12},{20,24},{24,20},{28,0},{0,28},{5,9},{9... | collective-permute-start | bytes 393224 | tf_op jit(solution)/shard_map/ppermute | solution.py:296
  17.5 0.1 pad_maximum_fusion.extended
  17.6 2.1 %first_modes.1 = (f32[4,64,128]{2,1,0:T(8,128)S(1)}, f32[4,64,128]{2,1,0:T(8,128)S(1)}, f32[4,64,128]{2,1,0:T(8,128)S(1)}, f32[4,64,128]{2,1,0:T(8,128)S(1)}) custom-call(s32[8,128]{1,0:T(8,128)S(1)} %get-tuple-element.31.moves, bf16[12,4,64,128]{3,2,1,0:T(8,128)(2,1)S(1)} %pad_maximum_fusion.extended, bf16[4,6,256,128]{3,2,1,0:T(8,128)(2,1)S(1)} %get-tuple-element.33.right, ...), custom_call_target="tpu_custom_call" | custom-call | flops 400000000 | bytes 1000000 | tf_op jit(solution)/shard_map/first_modes/pallas_call | solution.py:204
  19.8 1.1 %collective-permute-done.3.outer = bf16[2,4,64,128]{3,2,1,0:T(8,128)(2,1)S(1)} collective-permute-done((bf16[2,4,64,128]{3,2,1,0:T(8,128)(2,1)S(1)}, bf16[2,4,64,128]{3,2,1,0:T(8,128)(2,1)S(1)}, u32[]{:S(2)}, u32[]{:S(2)}) %collective-permute-start.3) | collective-permute-done | bytes 131104 | tf_op jit(solution)/shard_map/ppermute | solution.py:296
  20.9 1.7 %shard_map.64 = (bf16[4,64,128]{2,1,0:T(8,128)(2,1)S(1)}, bf16[4,64,128]{2,1,0:T(8,128)(2,1)S(1)}, bf16[4,64,128]{2,1,0:T(8,128)(2,1)S(1)}, bf16[4,64,128]{2,1,0:T(8,128)(2,1)S(1)}) custom-call(s32[8,128]{1,0:T(8,128)S(1)} %get-tuple-element.31.moves, bf16[2,4,64,128]{3,2,1,0:T(8,128)(2,1)S(1)} %collective-permute-done.3.outer, ...), custom_call_target="tpu_custom_call" | custom-call | flops 400000000 | bytes 1000000 | tf_op jit(solution)/shard_map/pallas_call | solution.py:251
  22.6 0.1 collective-permute-start.6
  22.7 2.6 %collective-permute-start.7 = (bf16[4,64,128]{2,1,0:T(8,128)(2,1)S(1)}, bf16[4,64,128]{2,1,0:T(8,128)(2,1)S(1)}, u32[]{:S(2)}, u32[]{:S(2)}) collective-permute-start(bf16[4,64,128]{2,1,0:T(8,128)(2,1)S(1)} %get-tuple-element.41), channel_id=1, source_target_pairs={{0,2},{1,3},{2,0},{3,1},{4,6},{5,7},{6,4},{7,5},{8,10},{9,11},{10,... | collective-permute-start | bytes 196616 | tf_op jit(solution)/shard_map/ppermute | solution.py:289
  25.3 1.8 %collective-permute-start.8 = (bf16[4,64,128]{2,1,0:T(8,128)(2,1)S(1)}, bf16[4,64,128]{2,1,0:T(8,128)(2,1)S(1)}, u32[]{:S(2)}, u32[]{:S(2)}) collective-permute-start(bf16[4,64,128]{2,1,0:T(8,128)(2,1)S(1)} %get-tuple-element.42), channel_id=1, source_target_pairs={{0,3},{1,2},{2,1},{3,0},{4,7},{5,6},{6,5},{7,4},{8,11},{9,10},{10,... | collective-permute-start | bytes 196616 | tf_op jit(solution)/shard_map/ppermute | solution.py:289
  27.0 1.1 %collective-permute-done.6.refs_1_ = bf16[4,64,128]{2,1,0:T(8,128)(2,1)S(1)} collective-permute-done((bf16[4,64,128]{2,1,0:T(8,128)(2,1)S(1)}, bf16[4,64,128]{2,1,0:T(8,128)(2,1)S(1)}, u32[]{:S(2)}, u32[]{:S(2)}) %collective-permute-start.6) | collective-permute-done | bytes 65568 | tf_op jit(solution)/shard_map/ppermute | solution.py:289
  28.1 2.1 %collective-permute-done.7.refs_2_ = bf16[4,64,128]{2,1,0:T(8,128)(2,1)S(1)} collective-permute-done((bf16[4,64,128]{2,1,0:T(8,128)(2,1)S(1)}, bf16[4,64,128]{2,1,0:T(8,128)(2,1)S(1)}, u32[]{:S(2)}, u32[]{:S(2)}) %collective-permute-start.7) | collective-permute-done | bytes 65568 | tf_op jit(solution)/shard_map/ppermute | solution.py:289
  30.3 1.2 %collective-permute-done.8.refs_3_ = bf16[4,64,128]{2,1,0:T(8,128)(2,1)S(1)} collective-permute-done((bf16[4,64,128]{2,1,0:T(8,128)(2,1)S(1)}, bf16[4,64,128]{2,1,0:T(8,128)(2,1)S(1)}, u32[]{:S(2)}, u32[]{:S(2)}) %collective-permute-start.8) | collective-permute-done | bytes 65568 | tf_op jit(solution)/shard_map/ppermute | solution.py:289
  31.4 0.7 %join.1 = bf16[1,16,64,128]{3,2,1,0:T(8,128)(2,1)} custom-call(bf16[4,64,128]{2,1,0:T(8,128)(2,1)S(1)} %get-tuple-element.39.refs_0_, bf16[4,64,128]{2,1,0:T(8,128)(2,1)S(1)} %collective-permute-done.6.refs_1_, bf16[4,64,128]{2,1,0:T(8,128)(2,1)S(1)} %collective-permute-done.7.refs_2_, bf16[4,64,128]{2,1,0:T(8,128)(2,1)S(1)} %collective-permute-done.8.refs_3_), custom_call_target="tpu_custom_call" | custom-call | tf_op jit(solution)/shard_map/join/pallas_call | solution.py:277
  (18 shorter events, 0.1 us)
Async XLA Ops:
  0.0 0.7 %copy-start.3 = (s32[16,2]{0,1:T(2,128)S(1)}, s32[16,2]{0,1:T(2,128)}, u32[]{:S(2)}) copy-start(s32[16,2]{0,1:T(2,128)} %param.8) | copy-start | bytes 388
  0.0 1.1 %copy-start = (bf16[1,16,3,64,128]{4,3,2,1,0:T(8,128)(2,1)S(1)}, bf16[1,16,3,64,128]{4,3,2,1,0:T(8,128)(2,1)}, u32[]{:S(2)}) copy-start(bf16[1,16,3,64,128]{4,3,2,1,0:T(8,128)(2,1)} %green.1) | copy-start | bytes 2359300
  0.0 1.2 %copy-start.2 = (bf16[1,16,64,128]{3,2,1,0:T(8,128)(2,1)S(1)}, bf16[1,16,64,128]{3,2,1,0:T(8,128)(2,1)}, u32[]{:S(2)}) copy-start(bf16[1,16,64,128]{3,2,1,0:T(8,128)(2,1)} %sigma.1) | copy-start | bytes 786436
  0.0 8.6 %copy-start.4 = (f32[6]{0:T(128)S(1)}, f32[6]{0:T(128)}, u32[]{:S(2)}) copy-start(f32[6]{0:T(128)} %occupancy.1) | copy-start | bytes 76
  0.0 8.6 %copy-start.5 = (s32[6]{0:T(128)S(1)}, s32[6]{0:T(128)}, u32[]{:S(2)}) copy-start(s32[6]{0:T(128)} %shifts.1) | copy-start | bytes 76
  0.0 8.6 %copy-start.1 = (bf16[6,4,64,128]{3,2,1,0:T(8,128)(2,1)S(1)}, bf16[6,4,64,128]{3,2,1,0:T(8,128)(2,1)}, u32[]{:S(2)}) copy-start(bf16[6,4,64,128]{3,2,1,0:T(8,128)(2,1)} %couplings.1) | copy-start | bytes 1179652
  2.9 7.2 %collective-permute-start = (bf16[4,64,128]{2,1,0:T(8,128)(2,1)S(1)}, bf16[4,64,128]{2,1,0:T(8,128)(2,1)S(1)}, u32[]{:S(2)}, u32[]{:S(2)}) collective-permute-start(bf16[4,64,128]{2,1,0:T(8,128)(2,1)S(1)} %get-tuple-element.25), channel_id=1, source_target_pairs={{0,1},{1,0},{2,3},{3,2},{4,5},{5,4},{6,7},{7,6},{8,9},{9,8},{10,11... | collective-permute-start | bytes 196616 | tf_op jit(solution)/shard_map/ppermute | solution.py:289
  6.0 7.3 %collective-permute-start.1 = (bf16[4,64,128]{2,1,0:T(8,128)(2,1)S(1)}, bf16[4,64,128]{2,1,0:T(8,128)(2,1)S(1)}, u32[]{:S(2)}, u32[]{:S(2)}) collective-permute-start(bf16[4,64,128]{2,1,0:T(8,128)(2,1)S(1)} %get-tuple-element.26), channel_id=1, source_target_pairs={{0,2},{1,3},{2,0},{3,1},{4,6},{5,7},{6,4},{7,5},{8,10},{9,11},{10,... | collective-permute-start | bytes 196616 | tf_op jit(solution)/shard_map/ppermute | solution.py:289
  8.6 6.1 %collective-permute-start.2 = (bf16[4,64,128]{2,1,0:T(8,128)(2,1)S(1)}, bf16[4,64,128]{2,1,0:T(8,128)(2,1)S(1)}, u32[]{:S(2)}, u32[]{:S(2)}) collective-permute-start(bf16[4,64,128]{2,1,0:T(8,128)(2,1)S(1)} %get-tuple-element.27), channel_id=1, source_target_pairs={{0,3},{1,2},{2,1},{3,0},{4,7},{5,6},{6,5},{7,4},{8,11},{9,10},{10,... | collective-permute-start | bytes 196616 | tf_op jit(solution)/shard_map/ppermute | solution.py:289
  10.1 7.3 %collective-permute-start.5 = (bf16[2,4,64,128]{3,2,1,0:T(8,128)(2,1)S(1)}, bf16[2,4,64,128]{3,2,1,0:T(8,128)(2,1)S(1)}, u32[]{:S(2)}, u32[]{:S(2)}) collective-permute-start(bf16[2,4,64,128]{3,2,1,0:T(8,128)(2,1)S(1)} %pad_maximum_fusion.2), channel_id=1, source_target_pairs={{4,8},{8,4},{12,16},{16,12},{20,24},{24,20},{28,0},{0,28},{5,9},{9... | collective-permute-start | bytes 393224 | tf_op jit(solution)/shard_map/ppermute | solution.py:296
  14.7 2.7 %collective-permute-start.4 = (bf16[4,4,64,128]{3,2,1,0:T(8,128)(2,1)S(1)}, bf16[4,4,64,128]{3,2,1,0:T(8,128)(2,1)S(1)}, u32[]{:S(2)}, u32[]{:S(2)}) collective-permute-start(bf16[4,4,64,128]{3,2,1,0:T(8,128)(2,1)S(1)} %pad_maximum_fusion.1), channel_id=1, source_target_pairs={{0,4},{4,0},{8,12},{12,8},{16,20},{20,16},{24,28},{28,24},{1,5},{5... | collective-permute-start | bytes 786440 | tf_op jit(solution)/shard_map/ppermute | solution.py:296
  14.8 6.0 %collective-permute-start.3 = (bf16[2,4,64,128]{3,2,1,0:T(8,128)(2,1)S(1)}, bf16[2,4,64,128]{3,2,1,0:T(8,128)(2,1)S(1)}, u32[]{:S(2)}, u32[]{:S(2)}) collective-permute-start(bf16[2,4,64,128]{3,2,1,0:T(8,128)(2,1)S(1)} %slice.3), channel_id=1, source_target_pairs={{4,8},{8,4},{12,16},{16,12},{20,24},{24,20},{28,0},{0,28},{5,9},{9... | collective-permute-start | bytes 393224 | tf_op jit(solution)/shard_map/ppermute | solution.py:296
  22.6 5.6 %collective-permute-start.6 = (bf16[4,64,128]{2,1,0:T(8,128)(2,1)S(1)}, bf16[4,64,128]{2,1,0:T(8,128)(2,1)S(1)}, u32[]{:S(2)}, u32[]{:S(2)}) collective-permute-start(bf16[4,64,128]{2,1,0:T(8,128)(2,1)S(1)} %get-tuple-element.40), channel_id=1, source_target_pairs={{0,1},{1,0},{2,3},{3,2},{4,5},{5,4},{6,7},{7,6},{8,9},{9,8},{10,11... | collective-permute-start | bytes 196616 | tf_op jit(solution)/shard_map/ppermute | solution.py:289
  22.7 7.6 %collective-permute-start.7 = (bf16[4,64,128]{2,1,0:T(8,128)(2,1)S(1)}, bf16[4,64,128]{2,1,0:T(8,128)(2,1)S(1)}, u32[]{:S(2)}, u32[]{:S(2)}) collective-permute-start(bf16[4,64,128]{2,1,0:T(8,128)(2,1)S(1)} %get-tuple-element.41), channel_id=1, source_target_pairs={{0,2},{1,3},{2,0},{3,1},{4,6},{5,7},{6,4},{7,5},{8,10},{9,11},{10,... | collective-permute-start | bytes 196616 | tf_op jit(solution)/shard_map/ppermute | solution.py:289
  25.3 6.2 %collective-permute-start.8 = (bf16[4,64,128]{2,1,0:T(8,128)(2,1)S(1)}, bf16[4,64,128]{2,1,0:T(8,128)(2,1)S(1)}, u32[]{:S(2)}, u32[]{:S(2)}) collective-permute-start(bf16[4,64,128]{2,1,0:T(8,128)(2,1)S(1)} %get-tuple-element.42), channel_id=1, source_target_pairs={{0,3},{1,2},{2,1},{3,0},{4,7},{5,6},{6,5},{7,4},{8,11},{9,10},{10,... | collective-permute-start | bytes 196616 | tf_op jit(solution)/shard_map/ppermute | solution.py:289

commit v5 on v4

--- a/solution.py
+++ b/solution.py
@@ -76,7 +76,7 @@
         me = lax.axis_index("eloc")
         copy = pltpu.make_async_copy(neighbours, table, done)
         copy.start()
-        spots = [(k, i, target_at(me, k, n) * per + i) for k in range(n - 1, -1, -1) for i in range(per)]
+        spots = [(k, i, target_at(me, k, n) * per + i) for k in range(n) for i in range(per)]
 
         def put_half(spot, j, other):
             k, i, atom = spot
@@ -198,6 +198,7 @@
                 ]
                 product = jnp.dot(jnp.concatenate(rows, 0), right[a, m], preferred_element_type=F32)
                 put_products(stack, a, m, product.astype(BF16), n, width)
+        for a in range(per):
             for k, piece in enumerate(outer_products(stack, left, a, n, width)):
                 outs[k][a] = piece
 
@@ -219,7 +220,7 @@
     width = 2 if count % 2 == 0 else 1
 
     def kernel(moves, outer, right, left, *rest):
-        partials, outs, stack = rest[:count], rest[count : 2 * count], rest[-1]
+        partials, outs, (made, stack) = rest[:count], rest[count : 2 * count], rest[2 * count :]
         me = lax.axis_index("eloc")
         even = lax.axis_index("egrp") & 1 == 0
         group = lax.axis_index("egrp")
@@ -236,15 +237,23 @@
                 slot = jnp.where(outside, place_of(me, t, n) - base, 0)
                 places[m, k] = (slot >= late, jnp.maximum(slot - late, 0))
         for a in range(per):
+            blocks = jnp.concatenate([outer[b, a] for b in range(n - late)], 0)
+            for m in range(0, modes, 2):
+                both = [right[a, m + i, pl.ds(begin, wide)] for i in range(min(2, modes - m))]
+                product = jnp.dot(blocks, jnp.concatenate(both, 1), preferred_element_type=F32).astype(BF16)
+                for i in range(len(both)):
+                    for b in range(n - late):
+                        made[a, b, m + i] = product[b * orb : (b + 1) * orb, i * wide : (i + 1) * wide]
+        for a in range(per):
             for m in range(modes):
-                rows = []
-                for k in ks:
+                for q, k in enumerate(ks):
                     held, slot = places[m, k]
-                    block = outer[slot, a]
-                    rows.append(jnp.where(held, block, jnp.zeros_like(block)))
-                weights = right[a, m, pl.ds(begin, wide)]
-                product = jnp.dot(jnp.concatenate(rows, 0), weights, preferred_element_type=F32)
-                put_products(stack, a, m, product.astype(BF16), count, width)
+                    block = made[a, slot, m]
+                    p, w = divmod(q, width)
+                    stack[a, p, m * orb : (m + 1) * orb, w * wide : (w + 1) * wide] = jnp.where(
+                        held, block, jnp.zeros_like(block)
+                    )
+        for a in range(per):
             for q, piece in enumerate(outer_products(stack, left, a, count, width)):
                 outs[q][a] = (partials[q][a] + piece).astype(BF16)
 
@@ -253,7 +262,10 @@
         out_shape=[jax.ShapeDtypeStruct((per, orb, wide), BF16) for _ in ks],
         in_specs=[VMEM for _ in range(4 + count)],
         out_specs=[VMEM for _ in ks],
-        scratch_shapes=[pltpu.VMEM((per, count // width, modes * orb, width * wide), BF16)],
+        scratch_shapes=[
+            pltpu.VMEM((per, n - late, modes, orb, wide), BF16),
+            pltpu.VMEM((per, count // width, modes * orb, width * wide), BF16),
+        ],
         compiler_params=limited(),
         cost_estimate=cost(400_000_000),
     )(moves, outer, right, left, *[partials[k] for k in ks])

time: 32.3 us -> 31.8 us (0.985)
  Pallas kernels: 7.71 us -> 6.69 us
  waiting for transfers between devices: 8.68 us -> 9.22 us
    pallas_call x1, Pallas kernels: 2.13 us -> 1.59 us  [first_modes(): pl.pallas_call(kernel, name='first_modes', out_shape=[jax.ShapeDtypeStruc...]
    ppermute x3, waiting for transfers between devices: 1.13 us -> 1.67 us  [traded(): return lax.ppermute(block, 'egrp', pairs)]
    pallas_call x1, Pallas kernels: 1.69 us -> 1.21 us  [last_modes(): pl.pallas_call(kernel, out_shape=[jax.ShapeDtypeStruct((per, orb, wide),...]
  transfers between devices with their start and end apart: 9 -> 9, of which waited for: 6 -> 6; matrix products, arithmetic and copies ran while one was open for 1% -> 1% of each run, Pallas kernels for 11% -> 10%
where the time goes in v5:
time: 31.8 us; the launch traced here: 31.7 us
  starting transfers between devices  14.2 us (45%)
  waiting for transfers between devices  9.22 us (29%)
  Pallas kernels  6.69 us (21%)
  local copies, waits for them, and re-layouts  1.21 us (4%)
    ppermute x6, starting transfers between devices, swapped(): lax.ppermute(block, 'eloc', [(i, partner(i, k, n)) for i in range(n)])  10.2 us
    ppermute x6, waiting for transfers between devices, swapped(): lax.ppermute(block, 'eloc', [(i, partner(i, k, n)) for i in range(n)])  7.56 us
    ppermute x3, starting transfers between devices, traded(): return lax.ppermute(block, 'egrp', pairs)  4.06 us
    pallas_call x1, Pallas kernels, lesser_blocks(): pl.pallas_call(kernel, name='lesser', out_shape=[jax.ShapeDtypeStruct((pe...  1.71 us
    ppermute x3, waiting for transfers between devices, traded(): return lax.ppermute(block, 'egrp', pairs)  1.67 us
    pallas_call x1, Pallas kernels, first_modes(): pl.pallas_call(kernel, name='first_modes', out_shape=[jax.ShapeDtypeStruc...  1.59 us
    pallas_call x1, Pallas kernels, prepared(): pl.pallas_call(kernel, name='prepare', out_shape=[jax.ShapeDtypeStruct((p...  1.45 us
    pallas_call x1, Pallas kernels, last_modes(): pl.pallas_call(kernel, out_shape=[jax.ShapeDtypeStruct((per, orb, wide),...  1.21 us
  transfers between devices with their start and end apart: 9, of which 6 were waited for; matrix products, arithmetic and copies ran while one was open for 1% of the time, Pallas kernels for 10%

profile of v5, /device:TPU:0, one launch (start us, length us, event | category | flops | bytes accessed | tf_op | source)
XLA Modules:
  0.0 31.7 jit_solution(11566181147145228807)
XLA Ops:
  0.0 0.6 %copy-done.3 = s32[16,2]{0,1:T(2,128)S(1)} copy-done((s32[16,2]{0,1:T(2,128)S(1)}, s32[16,2]{0,1:T(2,128)}, u32[]{:S(2)}) %copy-start.3) | copy-done | bytes 152
  0.7 0.5 %copy-done = bf16[1,16,3,64,128]{4,3,2,1,0:T(8,128)(2,1)S(1)} copy-done((bf16[1,16,3,64,128]{4,3,2,1,0:T(8,128)(2,1)S(1)}, bf16[1,16,3,64,128]{4,3,2,1,0:T(8,128)(2,1)}, u32[]{:S(2)}) %copy-start) | copy-done | bytes 786456
  1.1 0.1 copy-done.2
  1.2 1.7 %lesser.1 = (bf16[4,64,128]{2,1,0:T(8,128)(2,1)S(1)}, bf16[4,64,128]{2,1,0:T(8,128)(2,1)S(1)}, bf16[4,64,128]{2,1,0:T(8,128)(2,1)S(1)}, bf16[4,64,128]{2,1,0:T(8,128)(2,1)S(1)}) custom-call(s32[8,128]{1,0:T(8,128)S(1)} %opening.1, s32[2,16]{1,0:T(2,128)S(1)} %bitcast.7, bf16[1,16,3,64,128]{4,3,2,1,0:T(8,128)(2,1)S(1)} %copy-done, ...), custom_call_target="tpu_custom_call" | custom-call | flops 400000000 | bytes 1000000 | tf_op jit(solution)/shard_map/lesser/pallas_call | solution.py:101
  2.9 3.1 %collective-permute-start = (bf16[4,64,128]{2,1,0:T(8,128)(2,1)S(1)}, bf16[4,64,128]{2,1,0:T(8,128)(2,1)S(1)}, u32[]{:S(2)}, u32[]{:S(2)}) collective-permute-start(bf16[4,64,128]{2,1,0:T(8,128)(2,1)S(1)} %get-tuple-element.25), channel_id=1, source_target_pairs={{0,1},{1,0},{2,3},{3,2},{4,5},{5,4},{6,7},{7,6},{8,9},{9,8},{10,11... | collective-permute-start | bytes 196616 | tf_op jit(solution)/shard_map/ppermute | solution.py:301
  6.0 2.6 %collective-permute-start.1 = (bf16[4,64,128]{2,1,0:T(8,128)(2,1)S(1)}, bf16[4,64,128]{2,1,0:T(8,128)(2,1)S(1)}, u32[]{:S(2)}, u32[]{:S(2)}) collective-permute-start(bf16[4,64,128]{2,1,0:T(8,128)(2,1)S(1)} %get-tuple-element.26), channel_id=1, source_target_pairs={{0,2},{1,3},{2,0},{3,1},{4,6},{5,7},{6,4},{7,5},{8,10},{9,11},{10,... | collective-permute-start | bytes 196616 | tf_op jit(solution)/shard_map/ppermute | solution.py:301
  8.6 0.0 collective-permute-start.2
  8.6 1.5 %prepare.1 = (bf16[4,6,256,128]{3,2,1,0:T(8,128)(2,1)S(1)}, bf16[4,128,384]{2,1,0:T(8,128)(2,1)S(1)}, s32[8,128]{1,0:T(8,128)S(1)}) custom-call(f32[6]{0:T(128)S(1)} %copy-done.4, s32[6]{0:T(128)S(1)} %copy-done.5, bf16[6,4,64,128]{3,2,1,0:T(8,128)(2,1)S(1)} %copy-done.1), custom_call_target="tpu_custom_call" | custom-call | flops 200000000 | bytes 1000000 | tf_op jit(solution)/shard_map/prepare/pallas_call | solution.py:136
  10.1 1.4 %collective-permute-start.5 = (bf16[2,4,64,128]{3,2,1,0:T(8,128)(2,1)S(1)}, bf16[2,4,64,128]{3,2,1,0:T(8,128)(2,1)S(1)}, u32[]{:S(2)}, u32[]{:S(2)}) collective-permute-start(bf16[2,4,64,128]{3,2,1,0:T(8,128)(2,1)S(1)} %pad_maximum_fusion.2), channel_id=1, source_target_pairs={{4,8},{8,4},{12,16},{16,12},{20,24},{24,20},{28,0},{0,28},{5,9},{9... | collective-permute-start | bytes 393224 | tf_op jit(solution)/shard_map/ppermute | solution.py:308
  11.5 1.8 %collective-permute-done.1 = bf16[4,64,128]{2,1,0:T(8,128)(2,1)S(1)} collective-permute-done((bf16[4,64,128]{2,1,0:T(8,128)(2,1)S(1)}, bf16[4,64,128]{2,1,0:T(8,128)(2,1)S(1)}, u32[]{:S(2)}, u32[]{:S(2)}) %collective-permute-start.1) | collective-permute-done | bytes 65568 | tf_op jit(solution)/shard_map/ppermute | solution.py:301
  13.3 1.4 %collective-permute-done.2 = bf16[4,64,128]{2,1,0:T(8,128)(2,1)S(1)} collective-permute-done((bf16[4,64,128]{2,1,0:T(8,128)(2,1)S(1)}, bf16[4,64,128]{2,1,0:T(8,128)(2,1)S(1)}, u32[]{:S(2)}, u32[]{:S(2)}) %collective-permute-start.2) | collective-permute-done | bytes 65568 | tf_op jit(solution)/shard_map/ppermute | solution.py:301
  14.7 0.1 collective-permute-start.4
  14.8 2.6 %collective-permute-start.3 = (bf16[2,4,64,128]{3,2,1,0:T(8,128)(2,1)S(1)}, bf16[2,4,64,128]{3,2,1,0:T(8,128)(2,1)S(1)}, u32[]{:S(2)}, u32[]{:S(2)}) collective-permute-start(bf16[2,4,64,128]{3,2,1,0:T(8,128)(2,1)S(1)} %slice.3), channel_id=1, source_target_pairs={{4,8},{8,4},{12,16},{16,12},{20,24},{24,20},{28,0},{0,28},{5,9},{9... | collective-permute-start | bytes 393224 | tf_op jit(solution)/shard_map/ppermute | solution.py:308
  17.5 0.1 pad_maximum_fusion.extended
  17.6 1.6 %first_modes.1 = (f32[4,64,128]{2,1,0:T(8,128)S(1)}, f32[4,64,128]{2,1,0:T(8,128)S(1)}, f32[4,64,128]{2,1,0:T(8,128)S(1)}, f32[4,64,128]{2,1,0:T(8,128)S(1)}) custom-call(s32[8,128]{1,0:T(8,128)S(1)} %get-tuple-element.31.moves, bf16[12,4,64,128]{3,2,1,0:T(8,128)(2,1)S(1)} %pad_maximum_fusion.extended, bf16[4,6,256,128]{3,2,1,0:T(8,128)(2,1)S(1)} %get-tuple-element.33.right, ...), custom_call_target="tpu_custom_call" | custom-call | flops 400000000 | bytes 1000000 | tf_op jit(solution)/shard_map/first_modes/pallas_call | solution.py:205
  19.2 1.7 %collective-permute-done.3.outer = bf16[2,4,64,128]{3,2,1,0:T(8,128)(2,1)S(1)} collective-permute-done((bf16[2,4,64,128]{3,2,1,0:T(8,128)(2,1)S(1)}, bf16[2,4,64,128]{3,2,1,0:T(8,128)(2,1)S(1)}, u32[]{:S(2)}, u32[]{:S(2)}) %collective-permute-start.3) | collective-permute-done | bytes 131104 | tf_op jit(solution)/shard_map/ppermute | solution.py:308
  20.9 1.2 %shard_map.64 = (bf16[4,64,128]{2,1,0:T(8,128)(2,1)S(1)}, bf16[4,64,128]{2,1,0:T(8,128)(2,1)S(1)}, bf16[4,64,128]{2,1,0:T(8,128)(2,1)S(1)}, bf16[4,64,128]{2,1,0:T(8,128)(2,1)S(1)}) custom-call(s32[8,128]{1,0:T(8,128)S(1)} %get-tuple-element.31.moves, bf16[2,4,64,128]{3,2,1,0:T(8,128)(2,1)S(1)} %collective-permute-done.3.outer, ...), custom_call_target="tpu_custom_call" | custom-call | flops 400000000 | bytes 1000000 | tf_op jit(solution)/shard_map/pallas_call | solution.py:260
  22.1 0.1 collective-permute-start.6
  22.2 2.6 %collective-permute-start.7 = (bf16[4,64,128]{2,1,0:T(8,128)(2,1)S(1)}, bf16[4,64,128]{2,1,0:T(8,128)(2,1)S(1)}, u32[]{:S(2)}, u32[]{:S(2)}) collective-permute-start(bf16[4,64,128]{2,1,0:T(8,128)(2,1)S(1)} %get-tuple-element.41), channel_id=1, source_target_pairs={{0,2},{1,3},{2,0},{3,1},{4,6},{5,7},{6,4},{7,5},{8,10},{9,11},{10,... | collective-permute-start | bytes 196616 | tf_op jit(solution)/shard_map/ppermute | solution.py:301
  24.8 1.8 %collective-permute-start.8 = (bf16[4,64,128]{2,1,0:T(8,128)(2,1)S(1)}, bf16[4,64,128]{2,1,0:T(8,128)(2,1)S(1)}, u32[]{:S(2)}, u32[]{:S(2)}) collective-permute-start(bf16[4,64,128]{2,1,0:T(8,128)(2,1)S(1)} %get-tuple-element.42), channel_id=1, source_target_pairs={{0,3},{1,2},{2,1},{3,0},{4,7},{5,6},{6,5},{7,4},{8,11},{9,10},{10,... | collective-permute-start | bytes 196616 | tf_op jit(solution)/shard_map/ppermute | solution.py:301
  26.6 1.1 %collective-permute-done.6.refs_1_ = bf16[4,64,128]{2,1,0:T(8,128)(2,1)S(1)} collective-permute-done((bf16[4,64,128]{2,1,0:T(8,128)(2,1)S(1)}, bf16[4,64,128]{2,1,0:T(8,128)(2,1)S(1)}, u32[]{:S(2)}, u32[]{:S(2)}) %collective-permute-start.6) | collective-permute-done | bytes 65568 | tf_op jit(solution)/shard_map/ppermute | solution.py:301
  27.7 2.1 %collective-permute-done.7.refs_2_ = bf16[4,64,128]{2,1,0:T(8,128)(2,1)S(1)} collective-permute-done((bf16[4,64,128]{2,1,0:T(8,128)(2,1)S(1)}, bf16[4,64,128]{2,1,0:T(8,128)(2,1)S(1)}, u32[]{:S(2)}, u32[]{:S(2)}) %collective-permute-start.7) | collective-permute-done | bytes 65568 | tf_op jit(solution)/shard_map/ppermute | solution.py:301
  29.8 1.2 %collective-permute-done.8.refs_3_ = bf16[4,64,128]{2,1,0:T(8,128)(2,1)S(1)} collective-permute-done((bf16[4,64,128]{2,1,0:T(8,128)(2,1)S(1)}, bf16[4,64,128]{2,1,0:T(8,128)(2,1)S(1)}, u32[]{:S(2)}, u32[]{:S(2)}) %collective-permute-start.8) | collective-permute-done | bytes 65568 | tf_op jit(solution)/shard_map/ppermute | solution.py:301
  30.9 0.7 %join.1 = bf16[1,16,64,128]{3,2,1,0:T(8,128)(2,1)} custom-call(bf16[4,64,128]{2,1,0:T(8,128)(2,1)S(1)} %get-tuple-element.39.refs_0_, bf16[4,64,128]{2,1,0:T(8,128)(2,1)S(1)} %collective-permute-done.6.refs_1_, bf16[4,64,128]{2,1,0:T(8,128)(2,1)S(1)} %collective-permute-done.7.refs_2_, bf16[4,64,128]{2,1,0:T(8,128)(2,1)S(1)} %collective-permute-done.8.refs_3_), custom_call_target="tpu_custom_call" | custom-call | tf_op jit(solution)/shard_map/join/pallas_call | solution.py:289
  (18 shorter events, 0.1 us)
Async XLA Ops:
  0.0 0.7 %copy-start.3 = (s32[16,2]{0,1:T(2,128)S(1)}, s32[16,2]{0,1:T(2,128)}, u32[]{:S(2)}) copy-start(s32[16,2]{0,1:T(2,128)} %param.8) | copy-start | bytes 388
  0.0 1.1 %copy-start = (bf16[1,16,3,64,128]{4,3,2,1,0:T(8,128)(2,1)S(1)}, bf16[1,16,3,64,128]{4,3,2,1,0:T(8,128)(2,1)}, u32[]{:S(2)}) copy-start(bf16[1,16,3,64,128]{4,3,2,1,0:T(8,128)(2,1)} %green.1) | copy-start | bytes 2359300
  0.0 1.2 %copy-start.2 = (bf16[1,16,64,128]{3,2,1,0:T(8,128)(2,1)S(1)}, bf16[1,16,64,128]{3,2,1,0:T(8,128)(2,1)}, u32[]{:S(2)}) copy-start(bf16[1,16,64,128]{3,2,1,0:T(8,128)(2,1)} %sigma.1) | copy-start | bytes 786436
  0.0 8.6 %copy-start.4 = (f32[6]{0:T(128)S(1)}, f32[6]{0:T(128)}, u32[]{:S(2)}) copy-start(f32[6]{0:T(128)} %occupancy.1) | copy-start | bytes 76
  0.0 8.6 %copy-start.5 = (s32[6]{0:T(128)S(1)}, s32[6]{0:T(128)}, u32[]{:S(2)}) copy-start(s32[6]{0:T(128)} %shifts.1) | copy-start | bytes 76
  0.0 8.6 %copy-start.1 = (bf16[6,4,64,128]{3,2,1,0:T(8,128)(2,1)S(1)}, bf16[6,4,64,128]{3,2,1,0:T(8,128)(2,1)}, u32[]{:S(2)}) copy-start(bf16[6,4,64,128]{3,2,1,0:T(8,128)(2,1)} %couplings.1) | copy-start | bytes 1179652
  2.9 7.2 %collective-permute-start = (bf16[4,64,128]{2,1,0:T(8,128)(2,1)S(1)}, bf16[4,64,128]{2,1,0:T(8,128)(2,1)S(1)}, u32[]{:S(2)}, u32[]{:S(2)}) collective-permute-start(bf16[4,64,128]{2,1,0:T(8,128)(2,1)S(1)} %get-tuple-element.25), channel_id=1, source_target_pairs={{0,1},{1,0},{2,3},{3,2},{4,5},{5,4},{6,7},{7,6},{8,9},{9,8},{10,11... | collective-permute-start | bytes 196616 | tf_op jit(solution)/shard_map/ppermute | solution.py:301
  6.0 7.3 %collective-permute-start.1 = (bf16[4,64,128]{2,1,0:T(8,128)(2,1)S(1)}, bf16[4,64,128]{2,1,0:T(8,128)(2,1)S(1)}, u32[]{:S(2)}, u32[]{:S(2)}) collective-permute-start(bf16[4,64,128]{2,1,0:T(8,128)(2,1)S(1)} %get-tuple-element.26), channel_id=1, source_target_pairs={{0,2},{1,3},{2,0},{3,1},{4,6},{5,7},{6,4},{7,5},{8,10},{9,11},{10,... | collective-permute-start | bytes 196616 | tf_op jit(solution)/shard_map/ppermute | solution.py:301
  8.6 6.1 %collective-permute-start.2 = (bf16[4,64,128]{2,1,0:T(8,128)(2,1)S(1)}, bf16[4,64,128]{2,1,0:T(8,128)(2,1)S(1)}, u32[]{:S(2)}, u32[]{:S(2)}) collective-permute-start(bf16[4,64,128]{2,1,0:T(8,128)(2,1)S(1)} %get-tuple-element.27), channel_id=1, source_target_pairs={{0,3},{1,2},{2,1},{3,0},{4,7},{5,6},{6,5},{7,4},{8,11},{9,10},{10,... | collective-permute-start | bytes 196616 | tf_op jit(solution)/shard_map/ppermute | solution.py:301
  10.1 7.3 %collective-permute-start.5 = (bf16[2,4,64,128]{3,2,1,0:T(8,128)(2,1)S(1)}, bf16[2,4,64,128]{3,2,1,0:T(8,128)(2,1)S(1)}, u32[]{:S(2)}, u32[]{:S(2)}) collective-permute-start(bf16[2,4,64,128]{3,2,1,0:T(8,128)(2,1)S(1)} %pad_maximum_fusion.2), channel_id=1, source_target_pairs={{4,8},{8,4},{12,16},{16,12},{20,24},{24,20},{28,0},{0,28},{5,9},{9... | collective-permute-start | bytes 393224 | tf_op jit(solution)/shard_map/ppermute | solution.py:308
  14.7 2.7 %collective-permute-start.4 = (bf16[4,4,64,128]{3,2,1,0:T(8,128)(2,1)S(1)}, bf16[4,4,64,128]{3,2,1,0:T(8,128)(2,1)S(1)}, u32[]{:S(2)}, u32[]{:S(2)}) collective-permute-start(bf16[4,4,64,128]{3,2,1,0:T(8,128)(2,1)S(1)} %pad_maximum_fusion.1), channel_id=1, source_target_pairs={{0,4},{4,0},{8,12},{12,8},{16,20},{20,16},{24,28},{28,24},{1,5},{5... | collective-permute-start | bytes 786440 | tf_op jit(solution)/shard_map/ppermute | solution.py:308
  14.8 6.0 %collective-permute-start.3 = (bf16[2,4,64,128]{3,2,1,0:T(8,128)(2,1)S(1)}, bf16[2,4,64,128]{3,2,1,0:T(8,128)(2,1)S(1)}, u32[]{:S(2)}, u32[]{:S(2)}) collective-permute-start(bf16[2,4,64,128]{3,2,1,0:T(8,128)(2,1)S(1)} %slice.3), channel_id=1, source_target_pairs={{4,8},{8,4},{12,16},{16,12},{20,24},{24,20},{28,0},{0,28},{5,9},{9... | collective-permute-start | bytes 393224 | tf_op jit(solution)/shard_map/ppermute | solution.py:308
  22.1 5.6 %collective-permute-start.6 = (bf16[4,64,128]{2,1,0:T(8,128)(2,1)S(1)}, bf16[4,64,128]{2,1,0:T(8,128)(2,1)S(1)}, u32[]{:S(2)}, u32[]{:S(2)}) collective-permute-start(bf16[4,64,128]{2,1,0:T(8,128)(2,1)S(1)} %get-tuple-element.40), channel_id=1, source_target_pairs={{0,1},{1,0},{2,3},{3,2},{4,5},{5,4},{6,7},{7,6},{8,9},{9,8},{10,11... | collective-permute-start | bytes 196616 | tf_op jit(solution)/shard_map/ppermute | solution.py:301
  22.2 7.6 %collective-permute-start.7 = (bf16[4,64,128]{2,1,0:T(8,128)(2,1)S(1)}, bf16[4,64,128]{2,1,0:T(8,128)(2,1)S(1)}, u32[]{:S(2)}, u32[]{:S(2)}) collective-permute-start(bf16[4,64,128]{2,1,0:T(8,128)(2,1)S(1)} %get-tuple-element.41), channel_id=1, source_target_pairs={{0,2},{1,3},{2,0},{3,1},{4,6},{5,7},{6,4},{7,5},{8,10},{9,11},{10,... | collective-permute-start | bytes 196616 | tf_op jit(solution)/shard_map/ppermute | solution.py:301
  24.8 6.2 %collective-permute-start.8 = (bf16[4,64,128]{2,1,0:T(8,128)(2,1)S(1)}, bf16[4,64,128]{2,1,0:T(8,128)(2,1)S(1)}, u32[]{:S(2)}, u32[]{:S(2)}) collective-permute-start(bf16[4,64,128]{2,1,0:T(8,128)(2,1)S(1)} %get-tuple-element.42), channel_id=1, source_target_pairs={{0,3},{1,2},{2,1},{3,0},{4,7},{5,6},{6,5},{7,4},{8,11},{9,10},{10,... | collective-permute-start | bytes 196616 | tf_op jit(solution)/shard_map/ppermute | solution.py:301

commit v6 on v5

--- a/solution.py
+++ b/solution.py
@@ -76,7 +76,7 @@
         me = lax.axis_index("eloc")
         copy = pltpu.make_async_copy(neighbours, table, done)
         copy.start()
-        spots = [(k, i, target_at(me, k, n) * per + i) for k in range(n) for i in range(per)]
+        spots = [(k, i, target_at(me, k, n) * per + i) for k in range(n - 1, -1, -1) for i in range(per)]
 
         def put_half(spot, j, other):
             k, i, atom = spot
@@ -198,7 +198,6 @@
                 ]
                 product = jnp.dot(jnp.concatenate(rows, 0), right[a, m], preferred_element_type=F32)
                 put_products(stack, a, m, product.astype(BF16), n, width)
-        for a in range(per):
             for k, piece in enumerate(outer_products(stack, left, a, n, width)):
                 outs[k][a] = piece
 
@@ -324,7 +323,7 @@
     early = traded(groups, 1, soon)
     here = jnp.stack(held)
     here, right, left, moves = lax.optimization_barrier((here, right, left, moves))
-    outer = traded(groups, 1, here[n // 2 :])
+    outer = traded(groups, 1, jnp.stack(held[n // 2 :]))
     inner = traded(groups, 0, here)
     missing = jnp.zeros_like(outer)
     partials = first_modes(n, moves, jnp.concatenate([inner, here, inside(groups, early), missing], 0), right, left)

time: 31.8 us -> 31.9 us (level)
  Pallas kernels: 6.69 us -> 7.24 us
  waiting for transfers between devices: 9.22 us -> 8.68 us
    ppermute x3, waiting for transfers between devices: 1.67 us -> 1.11 us  [traded(): return lax.ppermute(block, 'egrp', pairs)]
    pallas_call x1, Pallas kernels: 1.59 us -> 2.13 us  [first_modes(): pl.pallas_call(kernel, name='first_modes', out_shape=[jax.ShapeDtypeStruc...]
  transfers between devices with their start and end apart: 9 -> 9, of which waited for: 6 -> 6; matrix products, arithmetic and copies ran while one was open for 1% -> 1% of each run, Pallas kernels for 10% -> 11%
where the time goes in v6:
time: 31.9 us; the launch traced here: 31.7 us
  starting transfers between devices  14.2 us (45%)
  waiting for transfers between devices  8.68 us (27%)
  Pallas kernels  7.24 us (23%)
  local copies, waits for them, and re-layouts  1.23 us (4%)
    ppermute x6, starting transfers between devices, swapped(): lax.ppermute(block, 'eloc', [(i, partner(i, k, n)) for i in range(n)])  10.2 us
    ppermute x6, waiting for transfers between devices, swapped(): lax.ppermute(block, 'eloc', [(i, partner(i, k, n)) for i in range(n)])  7.57 us
    ppermute x3, starting transfers between devices, traded(): return lax.ppermute(block, 'egrp', pairs)  4.07 us
    pallas_call x1, Pallas kernels, first_modes(): pl.pallas_call(kernel, name='first_modes', out_shape=[jax.ShapeDtypeStruc...  2.13 us
    pallas_call x1, Pallas kernels, lesser_blocks(): pl.pallas_call(kernel, name='lesser', out_shape=[jax.ShapeDtypeStruct((pe...  1.71 us
    pallas_call x1, Pallas kernels, prepared(): pl.pallas_call(kernel, name='prepare', out_shape=[jax.ShapeDtypeStruct((p...  1.45 us
    pallas_call x1, Pallas kernels, last_modes(): pl.pallas_call(kernel, out_shape=[jax.ShapeDtypeStruct((per, orb, wide),...  1.22 us
    unnamed x12, local copies, waits for them, and re-layouts  1.21 us
  transfers between devices with their start and end apart: 9, of which 6 were waited for; matrix products, arithmetic and copies ran while one was open for 1% of the time, Pallas kernels for 11%

profile of v6, /device:TPU:0, one launch (start us, length us, event | category | flops | bytes accessed | tf_op | source)
XLA Modules:
  0.0 31.7 jit_solution(5753533648255083806)
XLA Ops:
  0.0 0.6 %copy-done.3 = s32[16,2]{0,1:T(2,128)S(1)} copy-done((s32[16,2]{0,1:T(2,128)S(1)}, s32[16,2]{0,1:T(2,128)}, u32[]{:S(2)}) %copy-start.3) | copy-done | bytes 152
  0.7 0.3 copy-done.2
  1.0 0.3 copy-done
  1.2 1.7 %lesser.1 = (bf16[4,64,128]{2,1,0:T(8,128)(2,1)S(1)}, bf16[4,64,128]{2,1,0:T(8,128)(2,1)S(1)}, bf16[4,64,128]{2,1,0:T(8,128)(2,1)S(1)}, bf16[4,64,128]{2,1,0:T(8,128)(2,1)S(1)}) custom-call(s32[8,128]{1,0:T(8,128)S(1)} %opening.1, s32[2,16]{1,0:T(2,128)S(1)} %bitcast.7, bf16[1,16,3,64,128]{4,3,2,1,0:T(8,128)(2,1)S(1)} %copy-done, ...), custom_call_target="tpu_custom_call" | custom-call | flops 400000000 | bytes 1000000 | tf_op jit(solution)/shard_map/lesser/pallas_call | solution.py:101
  2.9 3.1 %collective-permute-start = (bf16[4,64,128]{2,1,0:T(8,128)(2,1)S(1)}, bf16[4,64,128]{2,1,0:T(8,128)(2,1)S(1)}, u32[]{:S(2)}, u32[]{:S(2)}) collective-permute-start(bf16[4,64,128]{2,1,0:T(8,128)(2,1)S(1)} %get-tuple-element.25), channel_id=1, source_target_pairs={{0,1},{1,0},{2,3},{3,2},{4,5},{5,4},{6,7},{7,6},{8,9},{9,8},{10,11... | collective-permute-start | bytes 196616 | tf_op jit(solution)/shard_map/ppermute | solution.py:300
  6.1 2.6 %collective-permute-start.1 = (bf16[4,64,128]{2,1,0:T(8,128)(2,1)S(1)}, bf16[4,64,128]{2,1,0:T(8,128)(2,1)S(1)}, u32[]{:S(2)}, u32[]{:S(2)}) collective-permute-start(bf16[4,64,128]{2,1,0:T(8,128)(2,1)S(1)} %get-tuple-element.26), channel_id=1, source_target_pairs={{0,2},{1,3},{2,0},{3,1},{4,6},{5,7},{6,4},{7,5},{8,10},{9,11},{10,... | collective-permute-start | bytes 196616 | tf_op jit(solution)/shard_map/ppermute | solution.py:300
  8.7 1.5 %prepare.1 = (bf16[4,6,256,128]{3,2,1,0:T(8,128)(2,1)S(1)}, bf16[4,128,384]{2,1,0:T(8,128)(2,1)S(1)}, s32[8,128]{1,0:T(8,128)S(1)}) custom-call(f32[6]{0:T(128)S(1)} %copy-done.4, s32[6]{0:T(128)S(1)} %copy-done.5, bf16[6,4,64,128]{3,2,1,0:T(8,128)(2,1)S(1)} %copy-done.1), custom_call_target="tpu_custom_call" | custom-call | flops 200000000 | bytes 1000000 | tf_op jit(solution)/shard_map/prepare/pallas_call | solution.py:136
  10.1 0.0 collective-permute-done
  10.2 1.4 %collective-permute-start.5 = (bf16[2,4,64,128]{3,2,1,0:T(8,128)(2,1)S(1)}, bf16[2,4,64,128]{3,2,1,0:T(8,128)(2,1)S(1)}, u32[]{:S(2)}, u32[]{:S(2)}) collective-permute-start(bf16[2,4,64,128]{3,2,1,0:T(8,128)(2,1)S(1)} %pad_maximum_fusion.3), channel_id=1, source_target_pairs={{4,8},{8,4},{12,16},{16,12},{20,24},{24,20},{28,0},{0,28},{5,9},{9... | collective-permute-start | bytes 393224 | tf_op jit(solution)/shard_map/ppermute | solution.py:307
  11.6 1.8 %collective-permute-done.1 = bf16[4,64,128]{2,1,0:T(8,128)(2,1)S(1)} collective-permute-done((bf16[4,64,128]{2,1,0:T(8,128)(2,1)S(1)}, bf16[4,64,128]{2,1,0:T(8,128)(2,1)S(1)}, u32[]{:S(2)}, u32[]{:S(2)}) %collective-permute-start.1) | collective-permute-done | bytes 65568 | tf_op jit(solution)/shard_map/ppermute | solution.py:300
  13.3 1.4 %collective-permute-done.2 = bf16[4,64,128]{2,1,0:T(8,128)(2,1)S(1)} collective-permute-done((bf16[4,64,128]{2,1,0:T(8,128)(2,1)S(1)}, bf16[4,64,128]{2,1,0:T(8,128)(2,1)S(1)}, u32[]{:S(2)}, u32[]{:S(2)}) %collective-permute-start.2) | collective-permute-done | bytes 65568 | tf_op jit(solution)/shard_map/ppermute | solution.py:300
  14.8 0.1 collective-permute-start.4
  14.9 2.6 %collective-permute-start.3 = (bf16[2,4,64,128]{3,2,1,0:T(8,128)(2,1)S(1)}, bf16[2,4,64,128]{3,2,1,0:T(8,128)(2,1)S(1)}, u32[]{:S(2)}, u32[]{:S(2)}) collective-permute-start(bf16[2,4,64,128]{3,2,1,0:T(8,128)(2,1)S(1)} %pad_maximum_fusion.2), channel_id=1, source_target_pairs={{4,8},{8,4},{12,16},{16,12},{20,24},{24,20},{28,0},{0,28},{5,9},{9... | collective-permute-start | bytes 393224 | tf_op jit(solution)/shard_map/ppermute | solution.py:307
  17.5 0.1 pad_maximum_fusion.extended
  17.7 2.1 %first_modes.1 = (f32[4,64,128]{2,1,0:T(8,128)S(1)}, f32[4,64,128]{2,1,0:T(8,128)S(1)}, f32[4,64,128]{2,1,0:T(8,128)S(1)}, f32[4,64,128]{2,1,0:T(8,128)S(1)}) custom-call(s32[8,128]{1,0:T(8,128)S(1)} %get-tuple-element.31.moves, bf16[12,4,64,128]{3,2,1,0:T(8,128)(2,1)S(1)} %pad_maximum_fusion.extended, bf16[4,6,256,128]{3,2,1,0:T(8,128)(2,1)S(1)} %get-tuple-element.32.right, ...), custom_call_target="tpu_custom_call" | custom-call | flops 400000000 | bytes 1000000 | tf_op jit(solution)/shard_map/first_modes/pallas_call | solution.py:204
  19.8 1.1 %collective-permute-done.3.outer = bf16[2,4,64,128]{3,2,1,0:T(8,128)(2,1)S(1)} collective-permute-done((bf16[2,4,64,128]{3,2,1,0:T(8,128)(2,1)S(1)}, bf16[2,4,64,128]{3,2,1,0:T(8,128)(2,1)S(1)}, u32[]{:S(2)}, u32[]{:S(2)}) %collective-permute-start.3) | collective-permute-done | bytes 131104 | tf_op jit(solution)/shard_map/ppermute | solution.py:307
  20.9 1.2 %shard_map.64 = (bf16[4,64,128]{2,1,0:T(8,128)(2,1)S(1)}, bf16[4,64,128]{2,1,0:T(8,128)(2,1)S(1)}, bf16[4,64,128]{2,1,0:T(8,128)(2,1)S(1)}, bf16[4,64,128]{2,1,0:T(8,128)(2,1)S(1)}) custom-call(s32[8,128]{1,0:T(8,128)S(1)} %get-tuple-element.31.moves, bf16[2,4,64,128]{3,2,1,0:T(8,128)(2,1)S(1)} %collective-permute-done.3.outer, ...), custom_call_target="tpu_custom_call" | custom-call | flops 400000000 | bytes 1000000 | tf_op jit(solution)/shard_map/pallas_call | solution.py:259
  22.1 0.1 collective-permute-start.6
  22.2 2.6 %collective-permute-start.7 = (bf16[4,64,128]{2,1,0:T(8,128)(2,1)S(1)}, bf16[4,64,128]{2,1,0:T(8,128)(2,1)S(1)}, u32[]{:S(2)}, u32[]{:S(2)}) collective-permute-start(bf16[4,64,128]{2,1,0:T(8,128)(2,1)S(1)} %get-tuple-element.41), channel_id=1, source_target_pairs={{0,2},{1,3},{2,0},{3,1},{4,6},{5,7},{6,4},{7,5},{8,10},{9,11},{10,... | collective-permute-start | bytes 196616 | tf_op jit(solution)/shard_map/ppermute | solution.py:300
  24.8 1.8 %collective-permute-start.8 = (bf16[4,64,128]{2,1,0:T(8,128)(2,1)S(1)}, bf16[4,64,128]{2,1,0:T(8,128)(2,1)S(1)}, u32[]{:S(2)}, u32[]{:S(2)}) collective-permute-start(bf16[4,64,128]{2,1,0:T(8,128)(2,1)S(1)} %get-tuple-element.42), channel_id=1, source_target_pairs={{0,3},{1,2},{2,1},{3,0},{4,7},{5,6},{6,5},{7,4},{8,11},{9,10},{10,... | collective-permute-start | bytes 196616 | tf_op jit(solution)/shard_map/ppermute | solution.py:300
  26.6 1.1 %collective-permute-done.6.refs_1_ = bf16[4,64,128]{2,1,0:T(8,128)(2,1)S(1)} collective-permute-done((bf16[4,64,128]{2,1,0:T(8,128)(2,1)S(1)}, bf16[4,64,128]{2,1,0:T(8,128)(2,1)S(1)}, u32[]{:S(2)}, u32[]{:S(2)}) %collective-permute-start.6) | collective-permute-done | bytes 65568 | tf_op jit(solution)/shard_map/ppermute | solution.py:300
  27.7 2.1 %collective-permute-done.7.refs_2_ = bf16[4,64,128]{2,1,0:T(8,128)(2,1)S(1)} collective-permute-done((bf16[4,64,128]{2,1,0:T(8,128)(2,1)S(1)}, bf16[4,64,128]{2,1,0:T(8,128)(2,1)S(1)}, u32[]{:S(2)}, u32[]{:S(2)}) %collective-permute-start.7) | collective-permute-done | bytes 65568 | tf_op jit(solution)/shard_map/ppermute | solution.py:300
  29.8 1.2 %collective-permute-done.8.refs_3_ = bf16[4,64,128]{2,1,0:T(8,128)(2,1)S(1)} collective-permute-done((bf16[4,64,128]{2,1,0:T(8,128)(2,1)S(1)}, bf16[4,64,128]{2,1,0:T(8,128)(2,1)S(1)}, u32[]{:S(2)}, u32[]{:S(2)}) %collective-permute-start.8) | collective-permute-done | bytes 65568 | tf_op jit(solution)/shard_map/ppermute | solution.py:300
  31.0 0.7 %join.1 = bf16[1,16,64,128]{3,2,1,0:T(8,128)(2,1)} custom-call(bf16[4,64,128]{2,1,0:T(8,128)(2,1)S(1)} %get-tuple-element.39.refs_0_, bf16[4,64,128]{2,1,0:T(8,128)(2,1)S(1)} %collective-permute-done.6.refs_1_, bf16[4,64,128]{2,1,0:T(8,128)(2,1)S(1)} %collective-permute-done.7.refs_2_, bf16[4,64,128]{2,1,0:T(8,128)(2,1)S(1)} %collective-permute-done.8.refs_3_), custom_call_target="tpu_custom_call" | custom-call | tf_op jit(solution)/shard_map/join/pallas_call | solution.py:288
  (18 shorter events, 0.1 us)
Async XLA Ops:
  0.0 0.7 %copy-start.3 = (s32[16,2]{0,1:T(2,128)S(1)}, s32[16,2]{0,1:T(2,128)}, u32[]{:S(2)}) copy-start(s32[16,2]{0,1:T(2,128)} %param.8) | copy-start | bytes 388
  0.0 1.0 %copy-start.2 = (bf16[1,16,64,128]{3,2,1,0:T(8,128)(2,1)S(1)}, bf16[1,16,64,128]{3,2,1,0:T(8,128)(2,1)}, u32[]{:S(2)}) copy-start(bf16[1,16,64,128]{3,2,1,0:T(8,128)(2,1)} %sigma.1) | copy-start | bytes 786436
  0.0 1.2 %copy-start = (bf16[1,16,3,64,128]{4,3,2,1,0:T(8,128)(2,1)S(1)}, bf16[1,16,3,64,128]{4,3,2,1,0:T(8,128)(2,1)}, u32[]{:S(2)}) copy-start(bf16[1,16,3,64,128]{4,3,2,1,0:T(8,128)(2,1)} %green.1) | copy-start | bytes 2359300
  0.0 8.6 %copy-start.5 = (s32[6]{0:T(128)S(1)}, s32[6]{0:T(128)}, u32[]{:S(2)}) copy-start(s32[6]{0:T(128)} %shifts.1) | copy-start | bytes 76
  0.0 8.7 %copy-start.4 = (f32[6]{0:T(128)S(1)}, f32[6]{0:T(128)}, u32[]{:S(2)}) copy-start(f32[6]{0:T(128)} %occupancy.1) | copy-start | bytes 76
  0.0 8.7 %copy-start.1 = (bf16[6,4,64,128]{3,2,1,0:T(8,128)(2,1)S(1)}, bf16[6,4,64,128]{3,2,1,0:T(8,128)(2,1)}, u32[]{:S(2)}) copy-start(bf16[6,4,64,128]{3,2,1,0:T(8,128)(2,1)} %couplings.1) | copy-start | bytes 1179652
  2.9 7.2 %collective-permute-start = (bf16[4,64,128]{2,1,0:T(8,128)(2,1)S(1)}, bf16[4,64,128]{2,1,0:T(8,128)(2,1)S(1)}, u32[]{:S(2)}, u32[]{:S(2)}) collective-permute-start(bf16[4,64,128]{2,1,0:T(8,128)(2,1)S(1)} %get-tuple-element.25), channel_id=1, source_target_pairs={{0,1},{1,0},{2,3},{3,2},{4,5},{5,4},{6,7},{7,6},{8,9},{9,8},{10,11... | collective-permute-start | bytes 196616 | tf_op jit(solution)/shard_map/ppermute | solution.py:300
  6.1 7.3 %collective-permute-start.1 = (bf16[4,64,128]{2,1,0:T(8,128)(2,1)S(1)}, bf16[4,64,128]{2,1,0:T(8,128)(2,1)S(1)}, u32[]{:S(2)}, u32[]{:S(2)}) collective-permute-start(bf16[4,64,128]{2,1,0:T(8,128)(2,1)S(1)} %get-tuple-element.26), channel_id=1, source_target_pairs={{0,2},{1,3},{2,0},{3,1},{4,6},{5,7},{6,4},{7,5},{8,10},{9,11},{10,... | collective-permute-start | bytes 196616 | tf_op jit(solution)/shard_map/ppermute | solution.py:300
  8.7 6.1 %collective-permute-start.2 = (bf16[4,64,128]{2,1,0:T(8,128)(2,1)S(1)}, bf16[4,64,128]{2,1,0:T(8,128)(2,1)S(1)}, u32[]{:S(2)}, u32[]{:S(2)}) collective-permute-start(bf16[4,64,128]{2,1,0:T(8,128)(2,1)S(1)} %get-tuple-element.27), channel_id=1, source_target_pairs={{0,3},{1,2},{2,1},{3,0},{4,7},{5,6},{6,5},{7,4},{8,11},{9,10},{10,... | collective-permute-start | bytes 196616 | tf_op jit(solution)/shard_map/ppermute | solution.py:300
  10.2 7.3 %collective-permute-start.5 = (bf16[2,4,64,128]{3,2,1,0:T(8,128)(2,1)S(1)}, bf16[2,4,64,128]{3,2,1,0:T(8,128)(2,1)S(1)}, u32[]{:S(2)}, u32[]{:S(2)}) collective-permute-start(bf16[2,4,64,128]{3,2,1,0:T(8,128)(2,1)S(1)} %pad_maximum_fusion.3), channel_id=1, source_target_pairs={{4,8},{8,4},{12,16},{16,12},{20,24},{24,20},{28,0},{0,28},{5,9},{9... | collective-permute-start | bytes 393224 | tf_op jit(solution)/shard_map/ppermute | solution.py:307
  14.8 2.7 %collective-permute-start.4 = (bf16[4,4,64,128]{3,2,1,0:T(8,128)(2,1)S(1)}, bf16[4,4,64,128]{3,2,1,0:T(8,128)(2,1)S(1)}, u32[]{:S(2)}, u32[]{:S(2)}) collective-permute-start(bf16[4,4,64,128]{3,2,1,0:T(8,128)(2,1)S(1)} %pad_maximum_fusion.1), channel_id=1, source_target_pairs={{0,4},{4,0},{8,12},{12,8},{16,20},{20,16},{24,28},{28,24},{1,5},{5... | collective-permute-start | bytes 786440 | tf_op jit(solution)/shard_map/ppermute | solution.py:307
  14.9 6.0 %collective-permute-start.3 = (bf16[2,4,64,128]{3,2,1,0:T(8,128)(2,1)S(1)}, bf16[2,4,64,128]{3,2,1,0:T(8,128)(2,1)S(1)}, u32[]{:S(2)}, u32[]{:S(2)}) collective-permute-start(bf16[2,4,64,128]{3,2,1,0:T(8,128)(2,1)S(1)} %pad_maximum_fusion.2), channel_id=1, source_target_pairs={{4,8},{8,4},{12,16},{16,12},{20,24},{24,20},{28,0},{0,28},{5,9},{9... | collective-permute-start | bytes 393224 | tf_op jit(solution)/shard_map/ppermute | solution.py:307
  22.1 5.6 %collective-permute-start.6 = (bf16[4,64,128]{2,1,0:T(8,128)(2,1)S(1)}, bf16[4,64,128]{2,1,0:T(8,128)(2,1)S(1)}, u32[]{:S(2)}, u32[]{:S(2)}) collective-permute-start(bf16[4,64,128]{2,1,0:T(8,128)(2,1)S(1)} %get-tuple-element.40), channel_id=1, source_target_pairs={{0,1},{1,0},{2,3},{3,2},{4,5},{5,4},{6,7},{7,6},{8,9},{9,8},{10,11... | collective-permute-start | bytes 196616 | tf_op jit(solution)/shard_map/ppermute | solution.py:300
  22.2 7.6 %collective-permute-start.7 = (bf16[4,64,128]{2,1,0:T(8,128)(2,1)S(1)}, bf16[4,64,128]{2,1,0:T(8,128)(2,1)S(1)}, u32[]{:S(2)}, u32[]{:S(2)}) collective-permute-start(bf16[4,64,128]{2,1,0:T(8,128)(2,1)S(1)} %get-tuple-element.41), channel_id=1, source_target_pairs={{0,2},{1,3},{2,0},{3,1},{4,6},{5,7},{6,4},{7,5},{8,10},{9,11},{10,... | collective-permute-start | bytes 196616 | tf_op jit(solution)/shard_map/ppermute | solution.py:300
  24.8 6.2 %collective-permute-start.8 = (bf16[4,64,128]{2,1,0:T(8,128)(2,1)S(1)}, bf16[4,64,128]{2,1,0:T(8,128)(2,1)S(1)}, u32[]{:S(2)}, u32[]{:S(2)}) collective-permute-start(bf16[4,64,128]{2,1,0:T(8,128)(2,1)S(1)} %get-tuple-element.42), channel_id=1, source_target_pairs={{0,3},{1,2},{2,1},{3,0},{4,7},{5,6},{6,5},{7,4},{8,11},{9,10},{10,... | collective-permute-start | bytes 196616 | tf_op jit(solution)/shard_map/ppermute | solution.py:300
